TPU v7x, 32 devices: a whole 2x2x4 slice. The times are simulated.
32 devices in a mesh: dp: 16 (over z, y, core), tensor: 2 (over x).
Axes of the slice: x: 2, y: 2, z: 4, core: 2. Of those that a mesh axis runs over, the one named last changes fastest.
Arguments:
- tokens: bfloat16 [21760, 1024], P('dp'), may hold values from -6 to 6
- d_out: bfloat16 [21760, 1024], P('dp'), may hold values from -6 to 6
- labels: int32 [32], replicated, may hold values from 0 to 999
- scale_ids: int32 [32, 680], P('dp'), may hold values from 0 to 9, never falling along the last dimension, each value on 1 to 256 neighbouring positions
- class_table: bfloat16 [1000, 1024], P(None, 'tensor'), may hold values from -6 to 6
- ada_weight: bfloat16 [1024, 6144], P(None, 'tensor'), may hold values from -0.1875 to 0.1875
- ada_bias: bfloat16 [6144], P('tensor'), may hold values from -3 to 3
- qkv_weight: bfloat16 [1024, 3, 1024], P(None, None, 'tensor'), may hold values from -0.1875 to 0.1875
- q_bias: bfloat16 [1024], P('tensor'), may hold values from -3 to 3
- v_bias: bfloat16 [1024], P('tensor'), may hold values from -3 to 3
- qk_scale: float32 [16], P('tensor'), may hold values from 2.3 to 3
- proj_weight: bfloat16 [1024, 1024], P('tensor'), may hold values from -0.75 to 0.75
- proj_bias: bfloat16 [1024], replicated, may hold values from -2 to 2
- fc1_weight: bfloat16 [1024, 4096], P(None, 'tensor'), may hold values from -0.1875 to 0.1875
- fc1_bias: bfloat16 [4096], P('tensor'), may hold values from -2 to 2
- fc2_weight: bfloat16 [4096, 1024], P('tensor'), may hold values from -0.1875 to 0.1875
- fc2_bias: bfloat16 [1024], replicated, may hold values from -2 to 2
Outputs:
- out: bfloat16 [21760, 1024], P('dp')
- d_tokens: bfloat16 [21760, 1024], P('dp')
- grad_table: float32 [1000, 1024], P(None, 'tensor')
- grad_ada: float32 [1024, 6144], P(None, 'tensor')
- grad_ada_bias: float32 [6144], P('tensor')
- grad_qkv: float32 [1024, 3, 1024], P(None, None, 'tensor')
- grad_q_bias: float32 [1024], P('tensor')
- grad_v_bias: float32 [1024], P('tensor')
- grad_qk_scale: float32 [16], P('tensor')
- grad_proj: float32 [1024, 1024], P('tensor')
- grad_proj_bias: float32 [1024], replicated
- grad_fc1: float32 [1024, 4096], P(None, 'tensor')
- grad_fc1_bias: float32 [4096], P('tensor')
- grad_fc2: float32 [4096, 1024], P('tensor')
- grad_fc2_bias: float32 [1024], replicated
Inputs may be any that keep to these rules, and one draw needn't show every extreme that they name: `scale_ids`: in each image the scale indices never fall, each of the 10 scales holds 1 to 256 tokens, and some scale of every image holds exactly 256.
All inputs are finite; a program needn't handle non-finite values.
Results may differ from a plain program's by a relative error of at most 0.033.
Values may be sent and summed in bfloat16 or wider, within the bound.
A program may use at most 320 MiB of HBM per device.

v0:
```python
from functools import partial

import jax
import jax.numpy as jnp
from jax import lax
from jax.sharding import PartitionSpec as P

epsilon = 1e-06
highest = lax.Precision.HIGHEST


def layer_stats(values):
    center = values - jnp.mean(values, axis=-1, keepdims=True)
    inv_std = lax.rsqrt(jnp.mean(center * center, axis=-1, keepdims=True) + epsilon)
    return (center * inv_std, inv_std)


def layer_back(d_normed, normed, inv_std):
    first_mean = jnp.mean(d_normed, axis=-1, keepdims=True)
    second_mean = jnp.mean(d_normed * normed, axis=-1, keepdims=True)
    return inv_std * (d_normed - first_mean - normed * second_mean)


def per_device(
    tokens,
    d_out,
    labels,
    scale_ids,
    class_table,
    ada_weight,
    ada_bias,
    qkv_weight,
    q_bias,
    v_bias,
    qk_scale,
    proj_weight,
    proj_bias,
    fc1_weight,
    fc1_bias,
    fc2_weight,
    fc2_bias,
):
    f32 = jnp.float32
    bf16 = jnp.bfloat16
    images = scale_ids.shape[0]
    length = scale_ids.shape[1]
    model_width = tokens.shape[1]
    rows_all = images * length
    classes = class_table.shape[0]
    heads_here = qk_scale.shape[0]
    local_width = qkv_weight.shape[2]
    head_size = local_width // heads_here
    mod_width = ada_weight.shape[1]
    first_image = lax.axis_index("dp") * images
    my_labels = lax.dynamic_slice_in_dim(labels, first_image, images)
    class_ids = jnp.arange(classes, dtype=jnp.int32)
    pick_mine = (my_labels[:, None] == class_ids[None, :]).astype(bf16)
    cond_cols = jnp.dot(pick_mine, class_table, preferred_element_type=f32)
    cond_full = lax.all_gather(cond_cols.astype(bf16), "tensor", axis=1, tiled=True)
    act_cond = jax.nn.silu(cond_full.astype(f32)).astype(bf16)
    mod_cols = jnp.dot(act_cond, ada_weight, preferred_element_type=f32) + ada_bias.astype(f32)
    modul = lax.all_gather(mod_cols, "tensor", axis=1, tiled=True)
    gain_one, gain_two, scale_one, scale_two, shift_one, shift_two = [
        modul[:, None, member * model_width : (member + 1) * model_width] for member in range(6)
    ]
    inputs = tokens.astype(f32).reshape(images, length, model_width)
    normed_one, inv_std_one = layer_stats(inputs)
    hidden_one = (
        (normed_one * (1.0 + scale_one) + shift_one).astype(bf16).reshape(rows_all, model_width)
    )
    bias_stack = jnp.stack([q_bias.astype(f32), jnp.zeros(q_bias.shape, f32), v_bias.astype(f32)])
    qkv_val = (
        jnp.einsum("rd,dpc->rpc", hidden_one, qkv_weight, preferred_element_type=f32)
        + bias_stack[None]
    )
    qkv_val = qkv_val.reshape(images, length, 3, heads_here, head_size)
    query_raw = qkv_val[:, :, 0]
    key_raw = qkv_val[:, :, 1]
    value_raw = qkv_val[:, :, 2]
    query_inv = lax.rsqrt(jnp.sum(query_raw * query_raw, axis=-1, keepdims=True) + epsilon)
    query_unit = query_raw * query_inv
    growth = jnp.exp(qk_scale)[None, None, :, None]
    query_scaled = query_unit * growth
    query_low = query_scaled.astype(bf16)
    key_inv = lax.rsqrt(jnp.sum(key_raw * key_raw, axis=-1, keepdims=True) + epsilon)
    key_unit = key_raw * key_inv
    key_low = key_unit.astype(bf16)
    value_low = value_raw.astype(bf16)
    allowed = scale_ids[:, None, None, :] <= scale_ids[:, None, :, None]

    def masked_scores():
        scores = jnp.einsum("ishe,ithe->ihst", query_low, key_low, preferred_element_type=f32)
        return jnp.where(allowed, scores, f32(-1e30))

    masked = masked_scores()
    row_max = jnp.max(masked, axis=-1, keepdims=True)
    weights_exp = jnp.exp(masked - row_max)
    row_total = jnp.sum(weights_exp, axis=-1, keepdims=True)
    log_total = row_max + jnp.log(row_total)
    probs_low = (weights_exp / row_total).astype(bf16)
    attn_out = (
        jnp.einsum("ihst,ithe->ishe", probs_low, value_low, preferred_element_type=f32)
        .reshape(rows_all, local_width)
        .astype(bf16)
    )
    gelu_tanh = partial(jax.nn.gelu, approximate=True)
    d_result = d_out.astype(f32).reshape(images, length, model_width)
    branch_one = lax.psum(jnp.dot(attn_out, proj_weight, preferred_element_type=f32), "tensor")
    branch_one = (branch_one + proj_bias.astype(f32)).reshape(images, length, model_width)
    middle = inputs + gain_one * branch_one
    normed_two, inv_std_two = layer_stats(middle)
    hidden_two = (
        (normed_two * (1.0 + scale_two) + shift_two).astype(bf16).reshape(rows_all, model_width)
    )
    pre_act = jnp.dot(hidden_two, fc1_weight, preferred_element_type=f32) + fc1_bias.astype(f32)
    mlp_low = gelu_tanh(pre_act).astype(bf16)
    branch_two = lax.psum(
        jnp.dot(mlp_low, fc2_weight, preferred_element_type=f32).astype(jnp.bfloat16), "tensor"
    ).astype(jnp.float32)
    branch_two = (branch_two + fc2_bias.astype(f32)).reshape(images, length, model_width)
    result = (middle + gain_two * branch_two).astype(bf16).reshape(rows_all, model_width)
    d_branch_two = (gain_two * d_result).astype(bf16).reshape(rows_all, model_width)
    grad_fc2 = jnp.einsum("rf,rd->fd", mlp_low, d_branch_two, preferred_element_type=f32)
    grad_fc2_bias = jnp.sum(d_branch_two.astype(f32), axis=0)
    d_mlp = jnp.einsum("rd,fd->rf", d_branch_two, fc2_weight, preferred_element_type=f32)
    gelu_value, gelu_pull = jax.vjp(gelu_tanh, pre_act)
    d_pre = gelu_pull(d_mlp)[0].astype(bf16)
    grad_fc1 = jnp.einsum("rd,rf->df", hidden_two, d_pre, preferred_element_type=f32)
    grad_fc1_bias = jnp.sum(d_pre.astype(f32), axis=0)
    d_hidden_two = lax.psum(
        jnp.einsum("rf,df->rd", d_pre, fc1_weight, preferred_element_type=f32), "tensor"
    )
    d_hidden_two = d_hidden_two.reshape(images, length, model_width)
    d_middle = d_result + layer_back(d_hidden_two * (1.0 + scale_two), normed_two, inv_std_two)
    d_branch_one = (gain_one * d_middle).astype(bf16).reshape(rows_all, model_width)
    grad_proj = jnp.einsum("rc,rd->cd", attn_out, d_branch_one, preferred_element_type=f32)
    grad_proj_bias = jnp.sum(d_branch_one.astype(f32), axis=0)
    d_attn = jnp.einsum("rd,cd->rc", d_branch_one, proj_weight, preferred_element_type=f32).astype(
        bf16
    )
    d_attn = d_attn.reshape(images, length, heads_here, head_size)
    again_probs = jnp.exp(masked_scores() - log_total)
    again_low = again_probs.astype(bf16)
    d_probs = jnp.einsum("ishe,ithe->ihst", d_attn, value_low, preferred_element_type=f32)
    d_scores = (
        again_probs * (d_probs - jnp.sum(again_probs * d_probs, axis=-1, keepdims=True))
    ).astype(bf16)
    d_query_scaled = jnp.einsum("ihst,ithe->ishe", d_scores, key_low, preferred_element_type=f32)
    d_key_unit = jnp.einsum("ihst,ishe->ithe", d_scores, query_low, preferred_element_type=f32)
    d_value = jnp.einsum("ihst,ishe->ithe", again_low, d_attn, preferred_element_type=f32)
    grad_scale = jnp.sum(d_query_scaled * query_scaled, axis=(0, 1, 3))
    d_query_unit = d_query_scaled * growth
    d_query = query_inv * (
        d_query_unit - query_unit * jnp.sum(d_query_unit * query_unit, axis=-1, keepdims=True)
    )
    d_key = key_inv * (
        d_key_unit - key_unit * jnp.sum(d_key_unit * key_unit, axis=-1, keepdims=True)
    )
    d_qkv = (
        jnp.stack([d_query, d_key, d_value], axis=2).reshape(rows_all, 3, local_width).astype(bf16)
    )
    grad_q_bias = jnp.sum(d_qkv[:, 0].astype(f32), axis=0)
    grad_v_bias = jnp.sum(d_qkv[:, 2].astype(f32), axis=0)
    grad_qkv = jnp.einsum("rd,rpc->dpc", hidden_one, d_qkv, preferred_element_type=f32)
    d_hidden_one = lax.psum(
        jnp.einsum("rpc,dpc->rd", d_qkv, qkv_weight, preferred_element_type=f32).astype(
            jnp.bfloat16
        ),
        "tensor",
    ).astype(jnp.float32)
    d_hidden_one = d_hidden_one.reshape(images, length, model_width)
    d_inputs = d_middle + layer_back(d_hidden_one * (1.0 + scale_one), normed_one, inv_std_one)
    d_tokens = d_inputs.astype(bf16).reshape(rows_all, model_width)
    d_modul = jnp.concatenate(
        [
            jnp.sum(d_middle * branch_one, axis=1),
            jnp.sum(d_result * branch_two, axis=1),
            jnp.sum(d_hidden_one * normed_one, axis=1),
            jnp.sum(d_hidden_two * normed_two, axis=1),
            jnp.sum(d_hidden_one, axis=1),
            jnp.sum(d_hidden_two, axis=1),
        ],
        axis=1,
    ).astype(bf16)
    col_start = lax.axis_index("tensor") * mod_width
    dmod_cols = lax.dynamic_slice_in_dim(d_modul, col_start, mod_width, 1)
    d_act_part = jnp.einsum("ic,dc->id", dmod_cols, ada_weight, preferred_element_type=f32)
    d_act_cols = lax.psum_scatter(d_act_part, "tensor", scatter_dimension=1, tiled=True)
    silu_value, silu_pull = jax.vjp(jax.nn.silu, cond_cols)
    d_cond = silu_pull(d_act_cols)[0]
    all_cond_grads = lax.all_gather(d_cond, "dp", axis=0, tiled=True)
    pick_all = (labels[:, None] == class_ids[None, :]).astype(f32)
    grad_table = jnp.einsum(
        "in,ic->nc", pick_all, all_cond_grads, precision=highest, preferred_element_type=f32
    )
    grad_ada, grad_ada_bias = (
        lax.psum(
            jnp.einsum("id,ic->dc", act_cond, dmod_cols, preferred_element_type=f32).astype(
                jnp.bfloat16
            ),
            "dp",
        ).astype(jnp.float32),
        lax.psum(jnp.sum(dmod_cols.astype(f32), axis=0).astype(jnp.bfloat16), "dp").astype(
            jnp.float32
        ),
    )
    (
        grad_qkv,
        grad_q_bias,
        grad_v_bias,
        grad_scale,
        grad_proj,
        grad_proj_bias,
        grad_fc1,
        grad_fc1_bias,
        grad_fc2,
        grad_fc2_bias,
    ) = (
        lax.psum(grad_qkv.astype(jnp.bfloat16), "dp").astype(jnp.float32),
        lax.psum(grad_q_bias.astype(jnp.bfloat16), "dp").astype(jnp.float32),
        lax.psum(grad_v_bias.astype(jnp.bfloat16), "dp").astype(jnp.float32),
        lax.psum(grad_scale.astype(jnp.bfloat16), "dp").astype(jnp.float32),
        lax.psum(grad_proj.astype(jnp.bfloat16), "dp").astype(jnp.float32),
        lax.psum(grad_proj_bias.astype(jnp.bfloat16), "dp").astype(jnp.float32),
        lax.psum(grad_fc1.astype(jnp.bfloat16), "dp").astype(jnp.float32),
        lax.psum(grad_fc1_bias.astype(jnp.bfloat16), "dp").astype(jnp.float32),
        lax.psum(grad_fc2.astype(jnp.bfloat16), "dp").astype(jnp.float32),
        lax.psum(grad_fc2_bias.astype(jnp.bfloat16), "dp").astype(jnp.float32),
    )
    return (
        result,
        d_tokens,
        grad_table,
        grad_ada,
        grad_ada_bias,
        grad_qkv,
        grad_q_bias,
        grad_v_bias,
        grad_scale,
        grad_proj,
        grad_proj_bias,
        grad_fc1,
        grad_fc1_bias,
        grad_fc2,
        grad_fc2_bias,
    )


def solution(mesh):
    return jax.shard_map(
        per_device,
        mesh=mesh,
        in_specs=(
            P("dp", None),
            P("dp", None),
            P(),
            P("dp", None),
            P(None, "tensor"),
            P(None, "tensor"),
            P("tensor"),
            P(None, None, "tensor"),
            P("tensor"),
            P("tensor"),
            P("tensor"),
            P("tensor", None),
            P(),
            P(None, "tensor"),
            P("tensor"),
            P("tensor", None),
            P(),
        ),
        out_specs=(
            P("dp", None),
            P("dp", None),
            P(None, "tensor"),
            P(None, "tensor"),
            P("tensor"),
            P(None, None, "tensor"),
            P("tensor"),
            P("tensor"),
            P("tensor"),
            P("tensor", None),
            P(),
            P(None, "tensor"),
            P("tensor"),
            P("tensor", None),
            P(),
        ),
        check_vma=False,
    )
```

profile of v0, /device:TPU:0, one launch (start us, length us, event | category | flops | bytes accessed | tf_op | source)
XLA Modules:
  0.0 1195.1 jit_solution(5245379113544800150)
XLA Ops:
  32.8 7.0 convolution_add_fusion
  39.8 12.8 %reshape.302 = f32[2,680,3,8,64]{4,3,1,0,2:T(8,128)} reshape(f32[1360,3,512]{2,0,1:T(8,128)} %convolution_add_fusion) | data formatting | bytes 16711680 | tf_op jit(solution)/shard_map/reshape | solution.py:76
  57.1 9.3 fusion.87
  80.5 5.9 copy.113
  88.7 16.8 %select_reduce_fusion = (f32[2,8,680]{2,1,0:T(8,128)S(1)}, f32[2,8,680,680]{2,3,1,0:T(8,128)}) fusion(pred[2,680,680]{1,2,0:T(8,128)(4,1)} %broadcast_compare_fusion, f32[2,680,1,8,64]{1,4,3,0,2:T(8,128)} %copy.113, f32[2,680,8]{1,2,0:T(8,128)S(1)} %get-tuple-element.73, f32[2,680,1,8,64]{1,4,3,0,2:T(8,128)} %copy.112, f32[8]{0:T(128)S(1)} %exp.18, ...), kind=kOutput, calls=%fused_computation.8 | convolution fusion | flops 965262720 | bytes 36219552 | tf_op jit(solution)/shard_map/ishe,ithe->ihst/dot_general | solution.py:92
  105.5 14.0 %fusion.2 = f32[2,8,680]{2,1,0:T(8,128)S(1)} fusion(f32[2,8,680,680]{2,3,1,0:T(8,128)} %get-tuple-element.64, f32[2,8,680]{2,1,0:T(8,128)S(1)} %get-tuple-element.63, pred[2,680,680]{1,2,0:T(8,128)(4,1)S(1)} %copy-done.9), kind=kLoop, calls=%fused_computation.7 | loop fusion | flops 22184320 | bytes 30605440 | tf_op jit(solution)/shard_map/reduce_sum | solution.py:98
  119.5 16.8 %fusion.51 = bf16[2,680,8,64]{1,3,2,0:T(8,128)(2,1)} fusion(f32[2,8,680,680]{2,3,1,0:T(8,128)} %get-tuple-element.64, f32[2,8,680]{2,1,0:T(8,128)S(1)} %fusion.2, f32[2,8,680]{2,1,0:T(8,128)S(1)} %get-tuple-element.63, pred[2,680,680]{1,2,0:T(8,128)(4,1)S(1)} %copy-done.9, bf16[2,680,1,8,64]{1,4,3,0,2:T(8,128)(2,1)} %copy.111), kind=kOutput, calls=%fused_computation.95 | convolution fusion | flops 977285120 | bytes 33390720 | tf_op jit(solution)/shard_map/ihst,ithe->ishe/dot_general | solution.py:102
  155.9 134.7 %all-reduce.8.cloned.1.call-done = f32[1360,1024]{1,0:T(8,128)} async-done(((f32[1360,1024]{1,0:T(8,128)}), f32[1360,1024]{1,0:T(8,128)}) %all-reduce.8.cloned.1.call-update) | async-done | bytes 5570576 | tf_op jit(solution)/shard_map/psum | solution.py:108
  290.6 6.5 bitcast_multiply_fusion.3
  301.9 8.9 fusion.92
  310.8 16.2 %fusion.82 = (bf16[2048]{0:T(1024)(128)(2,1)}, bf16[1360,2048]{1,0:T(8,128)(2,1)S(1)}) fusion(f32[1360,2048]{1,0:T(8,128)} %fusion.92, f32[2048]{0:T(1024)S(1)} %convert_element_type.187, bf16[1360,1024]{1,0:T(8,128)(2,1)S(1)} %copy-done.20, bf16[2048,1024]{1,0:T(8,128)(2,1)S(1)} %copy-done.62), kind=kOutput, calls=%fused_computation.149 | convolution fusion | flops 5765527552 | bytes 23703552 | tf_op jit(solution)/shard_map/rd,fd->rf/dot_general | solution.py:125
  329.4 7.9 fusion.93
  339.9 13.5 %convolution_convert_fusion.1 = bf16[1360,1024]{1,0:T(8,128)(2,1)} fusion(bf16[2048,1024]{1,0:T(8,128)(2,1)} %param.32, f32[1360,2048]{1,0:T(8,128)} %fusion.92, f32[2048]{0:T(1024)S(1)} %convert_element_type.187), kind=kOutput, calls=%fused_computation.56 | convolution fusion | flops 5733498880 | bytes 18128896 | tf_op jit(solution)/shard_map/dot_general | solution.py:118
  353.4 121.7 %all-reduce.10.cloned.1.call-done = f32[1360,1024]{1,0:T(8,128)} async-done(((f32[1360,1024]{1,0:T(8,128)}), f32[1360,1024]{1,0:T(8,128)}) %all-reduce.10.cloned.1.call-update) | async-done | bytes 5570576 | tf_op jit(solution)/shard_map/psum | solution.py:130
  478.3 9.2 fusion.79
  487.6 7.0 fusion.84
  507.8 17.4 %fusion.90 = (bf16[8,64]{1,0:T(8,128)(2,1)}, bf16[2,680,8,64]{1,3,2,0:T(8,128)(2,1)}) fusion(bf16[2,680,8,64]{1,3,2,0:T(8,128)(2,1)} %copy.84, f32[2,8,680,680]{2,3,1,0:T(8,128)} %get-tuple-element.64, f32[2,8,680]{2,1,0:T(8,128)S(1)} %log_add_fusion, pred[2,680,680]{1,2,0:T(8,128)(4,1)} %broadcast_compare_fusion), kind=kOutput, calls=%fused_computation.155 | convolution fusion | flops 970582528 | bytes 33348224 | tf_op jit(solution)/shard_map/ihst,ishe->ithe/dot_general | solution.py:150
  525.2 30.6 %multiply_reduce_fusion = (f32[2,8,680]{2,1,0:T(8,128)S(1)}, f32[2,8,680,680]{2,3,1,0:T(8,128)}) fusion(f32[2,8,680,680]{2,3,1,0:T(8,128)} %get-tuple-element.64, f32[2,8,680]{2,1,0:T(8,128)S(1)} %log_add_fusion, pred[2,680,680]{1,2,0:T(8,128)(4,1)} %broadcast_compare_fusion, bf16[2,680,8,64]{1,3,2,0:T(8,128)(2,1)} %copy.84, ...), kind=kOutput, calls=%fused_computation.3 | convolution fusion | flops 976577920 | bytes 62984320 | tf_op jit(solution)/shard_map/ishe,ithe->ihst/dot_general | solution.py:144
  555.8 28.4 %multiply_convert_fusion = bf16[2,8,680,680]{2,3,1,0:T(8,128)(2,1)} fusion(f32[2,8,680,680]{2,3,1,0:T(8,128)} %get-tuple-element.66, f32[2,8,680,680]{2,3,1,0:T(8,128)} %get-tuple-element.64, f32[2,8,680]{2,1,0:T(8,128)S(1)} %get-tuple-element.65, f32[2,8,680]{2,1,0:T(8,128)S(1)} %log_add_fusion, pred[2,680,680]{1,2,0:T(8,128)(4,1)} %broadcast_compare_fusion), kind=kLoop, calls=%fused_computation.2 | loop fusion | flops 36992000 | bytes 74995840 | tf_op jit(solution)/shard_map/convert_element_type | solution.py:147
  584.2 11.5 fusion.78
  595.7 10.3 fusion.25
  615.1 6.8 fusion.24
  653.5 11.2 convolution_convert_fusion.3
  664.9 13.3 %convolution_convert_fusion.2 = bf16[2048,1024]{1,0:T(8,128)(2,1)} fusion(bf16[1360,1024]{1,0:T(8,128)(2,1)} %get-tuple-element.40, f32[1360,2048]{1,0:T(8,128)} %fusion.92, f32[2048]{0:T(1024)S(1)} %convert_element_type.187), kind=kOutput, calls=%fused_computation.57 | convolution fusion | flops 5734203392 | bytes 18128896 | tf_op jit(solution)/shard_map/rf,rd->fd/dot_general | solution.py:123
  683.6 7.1 fusion.35
  690.7 100.6 %all-reduce.14.cloned.1.call-done = (bf16[1360,1024]{1,0:T(8,128)(2,1)}, bf16[1360,1024]{1,0:T(8,128)(2,1)}) async-done(((bf16[1360,1024]{1,0:T(8,128)(2,1)}, bf16[1360,1024]{1,0:T(8,128)(2,1)}), (bf16[1360,1024]{1,0:T(8,128)(2,1)}, bf16[1360,1024]{1,0:T(8,128)(2,1)})) %all-reduce.14.cloned.1.call-update) | async-done | bytes 5570576 | tf_op jit(solution)/shard_map/psum | solution.py:117
  791.4 6.4 convert_add_fusion
  797.8 9.9 multiply_reduce_fusion.1
  818.7 63.2 %all-reduce = (bf16[3072]{0:T(1024)(128)(2,1)S(1)}, bf16[512]{0:T(512)(128)(2,1)S(1)}, bf16[512]{0:T(512)(128)(2,1)S(1)}, bf16[8]{0:T(256)(128)(2,1)S(1)}, bf16[...) all-reduce(bf16[3072]{0:T(1024)(128)(2,1)S(1)} %fusion.73, ...), channel_id=1, replica_groups=mesh['dp'=16,'tensor'=2] {'dp'}, use_global_device_ids=true, to_apply=%region_28.29 | all-reduce | flops 8200 | bytes 32800 | tf_op jit(solution)/shard_map/psum | solution.py:203
  893.5 18.2 %all-gather = f32[16,2,512]{2,1,0:T(2,128)S(1)} all-gather(f32[1,2,512]{2,1,0:T(2,128)S(1)} %fusion.72), channel_id=1, replica_groups=mesh['dp'=16,'tensor'=2] {'dp'}, dimensions={0}, use_global_device_ids=true | all-gather | bytes 69632 | tf_op jit(solution)/shard_map/all_gather | solution.py:191
  914.2 249.5 %all-reduce.12.cloned.1.call-done = (bf16[1024,3072]{1,0:T(8,128)(2,1)}, bf16[1024,3,512]{2,0,1:T(8,128)(2,1)}, bf16[512,1024]{1,0:T(8,128)(2,1)}, bf16[1024,2048]{1,0:T(8,128)(2,1)}, bf16[2048,1024]{1,0:T(8,128)(2,1)}) async-done(((bf16[1024,3072]{1,0:T(8,128)(2,1)}, bf16[1024,3,512]{2,0,1:T(8,128)(2,1)}, bf16[512,1024]{1,0:T(8,128)(2,1)}, bf16[1024,2048]{1,0:T(8,128)(2,1)}, bf16[2048,1024]{1,0:T(8,128)(2,1)}), ...) | async-done | bytes 18874384 | tf_op jit(solution)/shard_map/psum | solution.py:197
  1166.5 9.4 convert_element_type.204
  (245 shorter events, 178.3 us)
Async XLA Ops:
  7.2 25.6 %copy-start = (bf16[1024,3,512]{2,0,1:T(8,128)(2,1)S(1)}, bf16[1024,3,512]{2,0,1:T(8,128)(2,1)}, u32[]{:S(2)}) copy-start(bf16[1024,3,512]{2,0,1:T(8,128)(2,1)} %param.24) | copy-start | bytes 9437188
  7.2 13.1 %copy-start.54 = (bf16[3072]{0:T(1024)(128)(2,1)S(1)}, bf16[3072]{0:T(1024)(128)(2,1)}, u32[]{:S(2)}) copy-start(bf16[3072]{0:T(1024)(128)(2,1)} %param.23) | copy-start | bytes 18436
  7.2 283.4 %all-reduce.8.cloned.1.call-start = ((), (), s32[]{:S(2)}) async-start(), calls=%async_computation.1 | async-start | bytes 11141120 | tf_op jit(solution)/shard_map/psum | solution.py:108
  8.8 10.5 copy-start.2
  19.3 11.9 copy-start.29
  20.3 11.0 copy-start.32
  28.5 122.5 %copy-start.43 = (f32[2,1024]{1,0:T(2,128)}, f32[2,1024]{1,0:T(2,128)S(1)}, u32[]{:S(2)}) copy-start(f32[2,1024]{1,0:T(2,128)S(1)} %get-tuple-element.57) | copy-start | bytes 24580
  28.5 446.6 %copy-start.39 = (f32[2,1024]{1,0:T(2,128)}, f32[2,1024]{1,0:T(2,128)S(1)}, u32[]{:S(2)}) copy-start(f32[2,1024]{1,0:T(2,128)S(1)} %get-tuple-element.55) | copy-start | bytes 24580
  28.5 459.0 %copy-start.37 = (f32[2,1024]{1,0:T(2,128)}, f32[2,1024]{1,0:T(2,128)S(1)}, u32[]{:S(2)}) copy-start(f32[2,1024]{1,0:T(2,128)S(1)} %get-tuple-element.60) | copy-start | bytes 24580
  57.1 9.3 copy-start.64
  57.1 9.3 copy-start.49
  66.4 22.3 %copy-start.35 = (f32[8]{0:T(128)}, f32[8]{0:T(128)S(1)}, u32[]{:S(2)}) copy-start(f32[8]{0:T(128)S(1)} %exp.18) | copy-start | bytes 100
  88.6 16.9 %copy-start.15 = (f32[2,680,8]{1,2,0:T(8,128)}, f32[2,680,8]{1,2,0:T(8,128)S(1)}, u32[]{:S(2)}) copy-start(f32[2,680,8]{1,2,0:T(8,128)S(1)} %get-tuple-element.74) | copy-start | bytes 130564
  88.6 16.8 %copy-start.25 = (f32[2,680,8]{1,2,0:T(8,128)}, f32[2,680,8]{1,2,0:T(8,128)S(1)}, u32[]{:S(2)}) copy-start(f32[2,680,8]{1,2,0:T(8,128)S(1)} %get-tuple-element.73) | copy-start | bytes 130564
  88.6 16.8 %copy-start.9 = (pred[2,680,680]{1,2,0:T(8,128)(4,1)S(1)}, pred[2,680,680]{1,2,0:T(8,128)(4,1)}, u32[]{:S(2)}) copy-start(pred[2,680,680]{1,2,0:T(8,128)(4,1)} %broadcast_compare_fusion) | copy-start | bytes 2774404
  150.9 324.2 %all-reduce.10.cloned.1.call-start = ((), (), s32[]{:S(2)}) async-start(), calls=%async_computation.2 | async-start | bytes 11141120 | tf_op jit(solution)/shard_map/psum | solution.py:130
  337.3 454.0 %all-reduce.14.cloned.1.call-start = ((), (), s32[]{:S(2)}) async-start(), calls=%async_computation.5 | async-start | bytes 11141120 | tf_op jit(solution)/shard_map/psum | solution.py:117
  475.1 12.5 %slice-start = ((s8[5570560]{0:T(1024)(128)(4,1)}), s8[4194304]{0:T(1024)(128)(4,1)S(1)}, s32[]{:S(2)}) async-start(s8[5570560]{0:T(1024)(128)(4,1)} %bitcast.175), calls=%async_computation.6 | async-start | bytes 8388608
  555.8 28.4 %copy-start.16 = (f32[2,680,8]{1,2,0:T(8,128)S(1)}, f32[2,680,8]{1,2,0:T(8,128)}, u32[]{:S(2)}) copy-start(f32[2,680,8]{1,2,0:T(8,128)} %copy-done.15) | copy-start | bytes 130564
  555.8 28.4 %copy-start.36 = (f32[8]{0:T(128)S(1)}, f32[8]{0:T(128)}, u32[]{:S(2)}) copy-start(f32[8]{0:T(128)} %copy-done.35) | copy-start | bytes 100
  584.1 11.5 copy-start.6
  584.2 11.5 copy-start.8
  584.2 11.5 copy-start.26
  653.5 239.0 %reduce-scatter.4.cloned.1.call-start = ((), (), s32[]{:S(2)}) async-start(), calls=%async_computation.3 | async-start | bytes 786432
  683.6 107.7 %copy-start.44 = (f32[2,1024]{1,0:T(2,128)S(1)}, f32[2,1024]{1,0:T(2,128)}, u32[]{:S(2)}) copy-start(f32[2,1024]{1,0:T(2,128)} %copy-done.43) | copy-start | bytes 24580
  683.6 107.7 %copy-start.51 = (f32[1024]{0:T(1024)S(1)}, f32[1024]{0:T(1024)}, u32[]{:S(2)}) copy-start(f32[1024]{0:T(1024)} %convert_element_type.191) | copy-start | bytes 12292
  813.2 350.5 %all-reduce.12.cloned.1.call-start = ((), (), s32[]{:S(2)}) async-start(), calls=%async_computation.4 | async-start | bytes 37748736 | tf_op jit(solution)/shard_map/psum | solution.py:197
  817.8 68.2 %copy-start.42 = (f32[2,1024]{1,0:T(2,128)S(1)}, f32[2,1024]{1,0:T(2,128)}, u32[]{:S(2)}) copy-start(f32[2,1024]{1,0:T(2,128)} %copy-done.41) | copy-start | bytes 24580
  817.9 68.9 %copy-start.31 = (f32[1360]{0:T(1024)S(1)}, f32[1360]{0:T(1024)}, u32[]{:S(2)}) copy-start(f32[1360]{0:T(1024)} %copy-done.29) | copy-start | bytes 16324
  817.9 68.9 %copy-start.34 = (f32[1360]{0:T(1024)S(1)}, f32[1360]{0:T(1024)}, u32[]{:S(2)}) copy-start(f32[1360]{0:T(1024)} %copy-done.32) | copy-start | bytes 16324
  888.9 22.9 %copy-start.60 = (s32[32]{0:T(128)S(1)}, s32[32]{0:T(128)}, u32[]{:S(2)}) copy-start(s32[32]{0:T(128)} %param.19) | copy-start | bytes 388
  1166.5 9.4 copy-start.19
  (43 other events, 194.9 us)
Sparse Core Ops, SparseCore 0:
  151.1 139.4 all-reduce.7
  337.4 137.6 all-reduce.9
  653.6 137.6 all-reduce.13
  813.3 14.6 reduce-scatter.3
  834.0 329.7 all-reduce.11
where the time goes:
time: 1200 us
  waiting for transfers between devices  607 us (51%)
  matrix products  226 us (19%)
  other arithmetic  148 us (12%)
  local copies, waits for them, and re-layouts  108 us (9%)
  blocking collectives  91.2 us (8%)
  between operations  14.8 us (1%)
    psum x1, waiting for transfers between devices, per_device(): lax.psum(jnp.einsum('id,ic->dc', act_cond, dmod_cols, preferred_element_t...  250 us
    psum x1, waiting for transfers between devices, per_device(): lax.psum(jnp.dot(attn_out, proj_weight, preferred_element_type=f32), 'ten...  135 us
    psum x1, waiting for transfers between devices, per_device(): lax.psum(jnp.einsum('rf,df->rd', d_pre, fc1_weight, preferred_element_typ...  122 us
    psum x1, waiting for transfers between devices, per_device(): lax.psum(jnp.dot(mlp_low, fc2_weight, preferred_element_type=f32).astype(...  101 us
    psum x1, blocking collectives, per_device(): lax.psum(jnp.sum(dmod_cols.astype(f32), axis=0).astype(jnp.bfloat16), 'dp')  63.2 us
    dot_general x1, matrix products, per_device(): jnp.einsum('ishe,ithe->ihst', d_attn, value_low, preferred_element_type=f32)  30.6 us
    unnamed x152, local copies, waits for them, and re-layouts  30.2 us
    convert_element_type x1, other arithmetic, per_device(): d_scores = (again_probs * (d_probs - jnp.sum(again_probs * d_probs, axis=...  28.4 us
  transfers between devices with their start and end apart: 5, of which 4 were waited for; matrix products, arithmetic and copies ran while one was open for 6% of the time, Pallas kernels for 0%

commit v1 on v0

--- a/solution.py
+++ b/solution.py
@@ -7,6 +7,13 @@
 
 epsilon = 1e-06
 highest = lax.Precision.HIGHEST
+
+
+def tensor_sum(part):
+    if lax.axis_size("tensor") == 2:
+        other = lax.ppermute(part, "tensor", [(0, 1), (1, 0)])
+        return part.astype(jnp.float32) + other.astype(jnp.float32)
+    return lax.psum(part, "tensor").astype(jnp.float32)
 
 
 def layer_stats(values):
@@ -52,11 +59,11 @@
     head_size = local_width // heads_here
     mod_width = ada_weight.shape[1]
     first_image = lax.axis_index("dp") * images
-    my_labels = lax.dynamic_slice_in_dim(labels, first_image, images)
     class_ids = jnp.arange(classes, dtype=jnp.int32)
-    pick_mine = (my_labels[:, None] == class_ids[None, :]).astype(bf16)
-    cond_cols = jnp.dot(pick_mine, class_table, preferred_element_type=f32)
-    cond_full = lax.all_gather(cond_cols.astype(bf16), "tensor", axis=1, tiled=True)
+    pick_all = labels[:, None] == class_ids[None, :]
+    cond_all_cols = jnp.dot(pick_all.astype(bf16), class_table, preferred_element_type=f32)
+    cond_all = lax.all_gather(cond_all_cols.astype(bf16), "tensor", axis=1, tiled=True)
+    cond_full = lax.dynamic_slice_in_dim(cond_all, first_image, images)
     act_cond = jax.nn.silu(cond_full.astype(f32)).astype(bf16)
     mod_cols = jnp.dot(act_cond, ada_weight, preferred_element_type=f32) + ada_bias.astype(f32)
     modul = lax.all_gather(mod_cols, "tensor", axis=1, tiled=True)
@@ -105,7 +112,7 @@
     )
     gelu_tanh = partial(jax.nn.gelu, approximate=True)
     d_result = d_out.astype(f32).reshape(images, length, model_width)
-    branch_one = lax.psum(jnp.dot(attn_out, proj_weight, preferred_element_type=f32), "tensor")
+    branch_one = tensor_sum(jnp.dot(attn_out, proj_weight, preferred_element_type=f32).astype(bf16))
     branch_one = (branch_one + proj_bias.astype(f32)).reshape(images, length, model_width)
     middle = inputs + gain_one * branch_one
     normed_two, inv_std_two = layer_stats(middle)
@@ -114,9 +121,7 @@
     )
     pre_act = jnp.dot(hidden_two, fc1_weight, preferred_element_type=f32) + fc1_bias.astype(f32)
     mlp_low = gelu_tanh(pre_act).astype(bf16)
-    branch_two = lax.psum(
-        jnp.dot(mlp_low, fc2_weight, preferred_element_type=f32).astype(jnp.bfloat16), "tensor"
-    ).astype(jnp.float32)
+    branch_two = tensor_sum(jnp.dot(mlp_low, fc2_weight, preferred_element_type=f32).astype(bf16))
     branch_two = (branch_two + fc2_bias.astype(f32)).reshape(images, length, model_width)
     result = (middle + gain_two * branch_two).astype(bf16).reshape(rows_all, model_width)
     d_branch_two = (gain_two * d_result).astype(bf16).reshape(rows_all, model_width)
@@ -127,8 +132,8 @@
     d_pre = gelu_pull(d_mlp)[0].astype(bf16)
     grad_fc1 = jnp.einsum("rd,rf->df", hidden_two, d_pre, preferred_element_type=f32)
     grad_fc1_bias = jnp.sum(d_pre.astype(f32), axis=0)
-    d_hidden_two = lax.psum(
-        jnp.einsum("rf,df->rd", d_pre, fc1_weight, preferred_element_type=f32), "tensor"
+    d_hidden_two = tensor_sum(
+        jnp.einsum("rf,df->rd", d_pre, fc1_weight, preferred_element_type=f32).astype(bf16)
     )
     d_hidden_two = d_hidden_two.reshape(images, length, model_width)
     d_middle = d_result + layer_back(d_hidden_two * (1.0 + scale_two), normed_two, inv_std_two)
@@ -162,12 +167,9 @@
     grad_q_bias = jnp.sum(d_qkv[:, 0].astype(f32), axis=0)
     grad_v_bias = jnp.sum(d_qkv[:, 2].astype(f32), axis=0)
     grad_qkv = jnp.einsum("rd,rpc->dpc", hidden_one, d_qkv, preferred_element_type=f32)
-    d_hidden_one = lax.psum(
-        jnp.einsum("rpc,dpc->rd", d_qkv, qkv_weight, preferred_element_type=f32).astype(
-            jnp.bfloat16
-        ),
-        "tensor",
-    ).astype(jnp.float32)
+    d_hidden_one = tensor_sum(
+        jnp.einsum("rpc,dpc->rd", d_qkv, qkv_weight, preferred_element_type=f32).astype(bf16)
+    )
     d_hidden_one = d_hidden_one.reshape(images, length, model_width)
     d_inputs = d_middle + layer_back(d_hidden_one * (1.0 + scale_one), normed_one, inv_std_one)
     d_tokens = d_inputs.astype(bf16).reshape(rows_all, model_width)
@@ -184,48 +186,30 @@
     ).astype(bf16)
     col_start = lax.axis_index("tensor") * mod_width
     dmod_cols = lax.dynamic_slice_in_dim(d_modul, col_start, mod_width, 1)
-    d_act_part = jnp.einsum("ic,dc->id", dmod_cols, ada_weight, preferred_element_type=f32)
+    dmod_all = lax.all_gather(dmod_cols, "dp", axis=0, tiled=True)
+    small = [grad_q_bias, grad_v_bias, grad_scale, grad_proj_bias, grad_fc1_bias, grad_fc2_bias]
+    sizes = [item.shape[0] for item in small]
+    packed = lax.all_gather(jnp.concatenate(small), "dp", axis=0, tiled=False)
+    packed = jnp.sum(packed, axis=0)
+    ends = [sum(sizes[: k + 1]) for k in range(len(sizes))]
+    grad_q_bias, grad_v_bias, grad_scale, grad_proj_bias, grad_fc1_bias, grad_fc2_bias = [
+        packed[e - n : e] for e, n in zip(ends, sizes)
+    ]
+    act_all = jax.nn.silu(cond_all.astype(f32)).astype(bf16)
+    d_act_part = jnp.einsum("ic,dc->id", dmod_all, ada_weight, preferred_element_type=f32)
     d_act_cols = lax.psum_scatter(d_act_part, "tensor", scatter_dimension=1, tiled=True)
-    silu_value, silu_pull = jax.vjp(jax.nn.silu, cond_cols)
+    silu_value, silu_pull = jax.vjp(jax.nn.silu, cond_all_cols)
     d_cond = silu_pull(d_act_cols)[0]
-    all_cond_grads = lax.all_gather(d_cond, "dp", axis=0, tiled=True)
-    pick_all = (labels[:, None] == class_ids[None, :]).astype(f32)
     grad_table = jnp.einsum(
-        "in,ic->nc", pick_all, all_cond_grads, precision=highest, preferred_element_type=f32
-    )
-    grad_ada, grad_ada_bias = (
-        lax.psum(
-            jnp.einsum("id,ic->dc", act_cond, dmod_cols, preferred_element_type=f32).astype(
-                jnp.bfloat16
-            ),
-            "dp",
-        ).astype(jnp.float32),
-        lax.psum(jnp.sum(dmod_cols.astype(f32), axis=0).astype(jnp.bfloat16), "dp").astype(
-            jnp.float32
-        ),
-    )
-    (
-        grad_qkv,
-        grad_q_bias,
-        grad_v_bias,
-        grad_scale,
-        grad_proj,
-        grad_proj_bias,
-        grad_fc1,
-        grad_fc1_bias,
-        grad_fc2,
-        grad_fc2_bias,
-    ) = (
-        lax.psum(grad_qkv.astype(jnp.bfloat16), "dp").astype(jnp.float32),
-        lax.psum(grad_q_bias.astype(jnp.bfloat16), "dp").astype(jnp.float32),
-        lax.psum(grad_v_bias.astype(jnp.bfloat16), "dp").astype(jnp.float32),
-        lax.psum(grad_scale.astype(jnp.bfloat16), "dp").astype(jnp.float32),
-        lax.psum(grad_proj.astype(jnp.bfloat16), "dp").astype(jnp.float32),
-        lax.psum(grad_proj_bias.astype(jnp.bfloat16), "dp").astype(jnp.float32),
-        lax.psum(grad_fc1.astype(jnp.bfloat16), "dp").astype(jnp.float32),
-        lax.psum(grad_fc1_bias.astype(jnp.bfloat16), "dp").astype(jnp.float32),
-        lax.psum(grad_fc2.astype(jnp.bfloat16), "dp").astype(jnp.float32),
-        lax.psum(grad_fc2_bias.astype(jnp.bfloat16), "dp").astype(jnp.float32),
+        "in,ic->nc", pick_all.astype(f32), d_cond, precision=highest, preferred_element_type=f32
+    )
+    grad_ada = jnp.einsum("id,ic->dc", act_all, dmod_all, preferred_element_type=f32)
+    grad_ada_bias = jnp.sum(dmod_all.astype(f32), axis=0)
+    grad_qkv, grad_proj, grad_fc1, grad_fc2 = (
+        lax.psum(grad_qkv.astype(bf16), "dp").astype(f32),
+        lax.psum(grad_proj.astype(bf16), "dp").astype(f32),
+        lax.psum(grad_fc1.astype(bf16), "dp").astype(f32),
+        lax.psum(grad_fc2.astype(bf16), "dp").astype(f32),
     )
     return (
         result,

time: 1200 us -> 920 us (0.77)
  waiting for transfers between devices: 607 us -> 376 us
  blocking collectives: 91.2 us -> 31.9 us
    psum x4 -> x1, waiting for transfers between devices: 607 us -> 214 us  [per_device(): lax.psum(grad_qkv.astype(bf16), 'dp').astype(f32)]
    ppermute x0 -> x4, waiting for transfers between devices: none -> 162 us  [tensor_sum(): other = lax.ppermute(part, 'tensor', [(0, 1), (1, 0)])]
    psum x1 -> x0, blocking collectives: 63.2 us -> none  [per_device(): lax.psum(jnp.sum(dmod_cols.astype(f32), axis=0).astype(jnp.bfloat16), 'dp')]
    convert_element_type x13 -> x4, other arithmetic: 32.2 us -> 17.3 us  [the longest x1 5.49 us: per_device(): lax.psum(grad_qkv.astype(bf16), 'dp').astype(f32)]
    unnamed x152 -> x125, local copies, waits for them, and re-layouts: 30.2 us -> 20.8 us
    dot_general x5 -> x6, matrix products: 28.3 us -> 32.4 us  [the longest x1 11.3 us: per_device(): jnp.dot(mlp_low, fc2_weight, preferred_element_type=f32).astype(bf16)]
    another operation x7 -> x6, local copies, waits for them, and re-layouts: 27.3 us -> 23.5 us  [per_device(): jnp.stack([d_query, d_key, d_value], axis=2)]
  transfers between devices with their start and end apart: 5 -> 7, of which waited for: 4 -> 4; matrix products, arithmetic and copies ran while one was open for 6% -> 14% of each run, Pallas kernels for 0% -> 0%
where the time goes in v1:
time: 920 us; the launch traced here: 914 us
  waiting for transfers between devices  376 us (41%)
  matrix products  232 us (25%)
  other arithmetic  144 us (16%)
  local copies, waits for them, and re-layouts  107 us (12%)
  blocking collectives  31.9 us (3%)
  between operations  17.4 us (2%)
    psum x1, waiting for transfers between devices, per_device(): lax.psum(grad_qkv.astype(bf16), 'dp').astype(f32)  214 us
    ppermute x4, waiting for transfers between devices, tensor_sum(): other = lax.ppermute(part, 'tensor', [(0, 1), (1, 0)])  162 us
    dot_general x1, matrix products, per_device(): jnp.einsum('ishe,ithe->ihst', d_attn, value_low, preferred_element_type=f32)  30.7 us
    convert_element_type x1, other arithmetic, per_device(): d_scores = (again_probs * (d_probs - jnp.sum(again_probs * d_probs, axis=...  28.4 us
    another operation x6, local copies, waits for them, and re-layouts, per_device(): jnp.stack([d_query, d_key, d_value], axis=2)  23.5 us
    all_gather x1, blocking collectives, per_device(): dmod_all = lax.all_gather(dmod_cols, 'dp', axis=0, tiled=True)  21.9 us
    unnamed x125, local copies, waits for them, and re-layouts  20.8 us
  transfers between devices with their start and end apart: 7, of which 4 were waited for; matrix products, arithmetic and copies ran while one was open for 14% of the time, Pallas kernels for 0%

profile of v1, /device:TPU:0, one launch (start us, length us, event | category | flops | bytes accessed | tf_op | source)
XLA Modules:
  0.0 914.1 jit_solution(17370807732758407328)
XLA Ops:
  33.7 6.9 convolution_add_fusion
  40.6 12.9 %reshape.303 = f32[2,680,3,8,64]{4,3,1,0,2:T(8,128)} reshape(f32[1360,3,512]{2,0,1:T(8,128)} %convolution_add_fusion) | data formatting | bytes 16711680 | tf_op jit(solution)/shard_map/reshape | solution.py:83
  58.0 9.3 %fusion.104 = (f32[2,680,1,8,64]{4,3,1,0,2:T(8,128)}, f32[2,680,1,8,64]{4,3,1,0,2:T(8,128)}) fusion(f32[2,680,3,8,64]{4,3,1,0,2:T(8,128)} %reshape.303), kind=kLoop, calls=%fused_computation.175 | loop fusion | bytes 11141120 | tf_op jit(solution)/shard_map/slice | solution.py:84
  81.4 6.0 copy.107
  89.7 16.8 %select_reduce_fusion = (f32[2,8,680]{2,1,0:T(8,128)S(1)}, f32[2,8,680,680]{2,3,1,0:T(8,128)}) fusion(pred[2,680,680]{1,2,0:T(8,128)(4,1)} %broadcast_compare_fusion, f32[2,680,1,8,64]{1,4,3,0,2:T(8,128)} %copy.107, f32[2,680,8]{1,2,0:T(8,128)S(1)} %get-tuple-element.67, f32[2,680,1,8,64]{1,4,3,0,2:T(8,128)} %copy.106, f32[8]{0:T(128)S(1)} %exp.22, ...), kind=kOutput, calls=%fused_computation.8 | convolution fusion | flops 965262720 | bytes 36219552 | tf_op jit(solution)/shard_map/ishe,ithe->ihst/dot_general | solution.py:99
  106.5 14.0 %fusion.2 = f32[2,8,680]{2,1,0:T(8,128)S(1)} fusion(f32[2,8,680,680]{2,3,1,0:T(8,128)} %get-tuple-element.62, f32[2,8,680]{2,1,0:T(8,128)S(1)} %get-tuple-element.61, pred[2,680,680]{1,2,0:T(8,128)(4,1)S(1)} %copy-done.8), kind=kLoop, calls=%fused_computation.7 | loop fusion | flops 22184320 | bytes 30605440 | tf_op jit(solution)/shard_map/reduce_sum | solution.py:105
  120.5 16.6 %fusion.51 = bf16[2,680,8,64]{1,3,2,0:T(8,128)(2,1)} fusion(f32[2,8,680,680]{2,3,1,0:T(8,128)} %get-tuple-element.62, f32[2,8,680]{2,1,0:T(8,128)S(1)} %fusion.2, f32[2,8,680]{2,1,0:T(8,128)S(1)} %get-tuple-element.61, pred[2,680,680]{1,2,0:T(8,128)(4,1)S(1)} %copy-done.8, bf16[2,680,1,8,64]{1,4,3,0,2:T(8,128)(2,1)} %copy.105), kind=kOutput, calls=%fused_computation.104 | convolution fusion | flops 977285120 | bytes 33390720 | tf_op jit(solution)/shard_map/ihst,ithe->ishe/dot_general | solution.py:109
  159.3 52.3 %collective-permute-done = bf16[1360,1024]{1,0:T(8,128)(2,1)} collective-permute-done((bf16[1360,1024]{1,0:T(8,128)(2,1)}, bf16[1360,1024]{1,0:T(8,128)(2,1)}, u32[]{:S(2)}, u32[]{:S(2)}) %collective-permute-start) | collective-permute-done | bytes 2785312 | tf_op jit(solution)/shard_map/ppermute | solution.py:14
  211.6 6.6 bitcast_multiply_fusion.3
  222.9 8.7 fusion.108
  231.7 11.3 %convolution_convert_fusion.1 = bf16[1360,1024]{1,0:T(8,128)(2,1)} fusion(bf16[2048,1024]{1,0:T(8,128)(2,1)S(1)} %copy-done.45, f32[1360,2048]{1,0:T(8,128)} %fusion.108, f32[2048]{0:T(1024)S(1)} %convert_element_type.198), kind=kOutput, calls=%fused_computation.63 | convolution fusion | flops 5733498880 | bytes 18128896 | tf_op jit(solution)/shard_map/dot_general | solution.py:124
  244.8 16.8 %convert_reduce_fusion = (f32[2048]{0:T(1024)}, bf16[1360,2048]{1,0:T(8,128)(2,1)}) fusion(f32[1360,2048]{1,0:T(8,128)} %fusion.108, f32[2048]{0:T(1024)S(1)} %convert_element_type.198, bf16[1360,1024]{1,0:T(8,128)(2,1)S(1)} %get-tuple-element.30, bf16[2048,1024]{1,0:T(8,128)(2,1)S(1)} %copy-done.45), kind=kOutput, calls=%fused_computation.24 | convolution fusion | flops 5768312832 | bytes 23707648 | tf_op jit(solution)/shard_map/rd,fd->rf/dot_general | solution.py:130
  261.6 10.0 %convolution_convert_fusion = bf16[1360,1024]{1,0:T(8,128)(2,1)} fusion(bf16[1360,2048]{1,0:T(8,128)(2,1)} %get-tuple-element.32, bf16[1024,2048]{1,0:T(8,128)(2,1)S(1)} %copy-done.46), kind=kOutput, calls=%fused_computation.62 | convolution fusion | flops 5705646080 | bytes 12550144 | tf_op jit(solution)/shard_map/rf,df->rd/dot_general | solution.py:136
  271.9 12.8 %convolution_convert_fusion.2 = bf16[2048,1024]{1,0:T(8,128)(2,1)} fusion(bf16[1360,1024]{1,0:T(8,128)(2,1)S(1)} %get-tuple-element.30, f32[1360,2048]{1,0:T(8,128)} %fusion.108, f32[2048]{0:T(1024)S(1)} %convert_element_type.198), kind=kOutput, calls=%fused_computation.64 | convolution fusion | flops 5734203392 | bytes 18128896 | tf_op jit(solution)/shard_map/rf,rd->fd/dot_general | solution.py:128
  284.9 77.4 %collective-permute-done.2 = bf16[1360,1024]{1,0:T(8,128)(2,1)} collective-permute-done((bf16[1360,1024]{1,0:T(8,128)(2,1)}, bf16[1360,1024]{1,0:T(8,128)(2,1)}, u32[]{:S(2)}, u32[]{:S(2)}) %collective-permute-start.2) | collective-permute-done | bytes 2785312 | tf_op jit(solution)/shard_map/ppermute | solution.py:14
  365.5 7.7 fusion.99
  373.3 12.9 %convert_reduce_fusion.2 = (f32[1024]{0:T(1024)S(1)}, bf16[1360,1024]{1,0:T(8,128)(2,1)}, f32[1360,1024]{1,0:T(8,128)}, f32[1360,1024]{1,0:T(8,128)}, bf16[1360,1024]{1,0:T(8,128)(2,1)}, /*index=5*/f32[1360,1024]{1,0:T(8,128)}) fusion(f32[2,1024]{1,0:T(2,128)S(1)} %get-tuple-element.54, f32[1360]{0:T(1024)S(1)} %broadcast_multiply_fusion.2, ...), kind=kLoop, calls=%fused_computation.40 | loop fusion | flops 32029696 | bytes 41833728 | tf_op jit(solution)/shard_map/reduce_sum | solution.py:142
  399.4 16.6 %fusion.48 = bf16[2,680,8,64]{1,3,2,0:T(8,128)(2,1)} fusion(bf16[2,680,8,64]{1,3,2,0:T(8,128)(2,1)} %copy.84, f32[2,8,680,680]{2,3,1,0:T(8,128)} %get-tuple-element.62, f32[2,8,680]{2,1,0:T(8,128)S(1)} %log_add_fusion, pred[2,680,680]{1,2,0:T(8,128)(4,1)} %broadcast_compare_fusion), kind=kOutput, calls=%fused_computation.102 | convolution fusion | flops 969886720 | bytes 33347200 | tf_op jit(solution)/shard_map/ihst,ishe->ithe/dot_general | solution.py:155
  416.1 30.7 %multiply_reduce_fusion = (f32[2,8,680]{2,1,0:T(8,128)S(1)}, f32[2,8,680,680]{2,3,1,0:T(8,128)}) fusion(f32[2,8,680,680]{2,3,1,0:T(8,128)} %get-tuple-element.62, f32[2,8,680]{2,1,0:T(8,128)S(1)} %log_add_fusion, pred[2,680,680]{1,2,0:T(8,128)(4,1)} %broadcast_compare_fusion, bf16[2,680,8,64]{1,3,2,0:T(8,128)(2,1)} %copy.84, ...), kind=kOutput, calls=%fused_computation.3 | convolution fusion | flops 976577920 | bytes 62984320 | tf_op jit(solution)/shard_map/ishe,ithe->ihst/dot_general | solution.py:149
  446.8 28.4 %multiply_convert_fusion = bf16[2,8,680,680]{2,3,1,0:T(8,128)(2,1)} fusion(f32[2,8,680,680]{2,3,1,0:T(8,128)} %get-tuple-element.64, f32[2,8,680,680]{2,3,1,0:T(8,128)} %get-tuple-element.62, f32[2,8,680]{2,1,0:T(8,128)S(1)} %get-tuple-element.63, f32[2,8,680]{2,1,0:T(8,128)S(1)} %log_add_fusion, pred[2,680,680]{1,2,0:T(8,128)(4,1)} %broadcast_compare_fusion), kind=kLoop, calls=%fused_computation.2 | loop fusion | flops 36992000 | bytes 74995840 | tf_op jit(solution)/shard_map/convert_element_type | solution.py:152
  475.2 11.5 %fusion.97 = f32[2,8,64,680]{3,2,1,0:T(8,128)} fusion(bf16[2,8,680,680]{2,3,1,0:T(8,128)(2,1)} %multiply_convert_fusion, f32[2,680,1,8,64]{1,4,3,0,2:T(8,128)} %copy.106, f32[8]{0:T(128)S(1)} %copy-done.31, f32[2,680,8]{1,2,0:T(8,128)S(1)} %copy-done.12), kind=kOutput, calls=%fused_computation.171 | convolution fusion | flops 949084160 | bytes 20410912 | tf_op jit(solution)/shard_map/ihst,ishe->ithe/dot_general | solution.py:154
  486.7 10.5 %fusion.25 = (f32[8]{0:T(128)S(1)}, f32[2,8,64,680]{3,2,1,0:T(8,128)}) fusion(f32[2,680,1,8,64]{1,4,3,0,2:T(8,128)S(1)} %copy-done.5, f32[8]{0:T(128)S(1)} %copy-done.31, f32[2,680,8]{1,2,0:T(8,128)S(1)} %copy-done.12, bf16[2,8,680,680]{2,3,1,0:T(8,128)(2,1)} %multiply_convert_fusion, f32[2,680,1,8,64]{1,4,3,0,2:T(8,128)S(1)} %copy-done.7, ...), kind=kOutput, calls=%fused_computation.74 | convolution fusion | flops 951173120 | bytes 23239744 | tf_op jit(solution)/shard_map/ihst,ithe->ishe/dot_general | solution.py:153
  507.2 6.8 fusion.24
  534.1 8.2 bitcast_convert_fusion
  543.7 11.0 %convolution_convert_fusion.3 = bf16[1024,2048]{1,0:T(8,128)(2,1)} fusion(bf16[1360,1024]{1,0:T(8,128)(2,1)S(1)} %copy-done.17, bf16[1360,2048]{1,0:T(8,128)(2,1)} %get-tuple-element.32), kind=kOutput, calls=%fused_computation.65 | convolution fusion | flops 5706350592 | bytes 12550144 | tf_op jit(solution)/shard_map/rd,rf->df/dot_general | solution.py:133
  559.6 9.5 %fusion.35 = bf16[1024,3,512]{2,0,1:T(8,128)(2,1)} fusion(bf16[1360,1024]{1,0:T(8,128)(2,1)} %copy-done.15, bf16[1360,1,512]{2,0,1:T(8,128)(2,1)} %copy.94, bf16[1360,1,512]{2,0,1:T(8,128)(2,1)} %reshape.302, bf16[1360,1,512]{2,0,1:T(8,128)(2,1)} %copy.92), kind=kOutput, calls=%fused_computation.92 | convolution fusion | flops 4292296704 | bytes 10108928 | tf_op jit(solution)/shard_map/rd,rpc->dpc/dot_general | solution.py:169
  569.1 31.9 %collective-permute-done.3 = bf16[1360,1024]{1,0:T(8,128)(2,1)} collective-permute-done((bf16[1360,1024]{1,0:T(8,128)(2,1)}, bf16[1360,1024]{1,0:T(8,128)(2,1)}, u32[]{:S(2)}, u32[]{:S(2)}) %collective-permute-start.3) | collective-permute-done | bytes 2785312 | tf_op jit(solution)/shard_map/ppermute | solution.py:14
  604.2 6.5 fusion.98
  616.3 9.5 %multiply_reduce_fusion.1 = (bf16[2,1024]{1,0:T(2,128)(2,1)S(1)}, bf16[2,1024]{1,0:T(2,128)(2,1)S(1)}, bf16[2,1024]{1,0:T(2,128)(2,1)S(1)}, bf16[2,1024]{1,0:T(2...) fusion(f32[2,680,1024]{2,1,0:T(8,128)} %bitcast.179, f32[2,680,1024]{2,1,0:T(8,128)S(1)} %bitcast.178, ...), kind=kLoop, calls=%fused_computation.41 | loop fusion | flops 33411072 | bytes 27926400 | tf_op jit(solution)/shard_map/reduce_sum | solution.py:181
  625.9 21.9 %all-gather.1 = bf16[16,2,3072]{2,1,0:T(2,128)(2,1)S(1)} all-gather(bf16[1,2,3072]{2,1,0:T(2,128)(2,1)S(1)} %dynamic-slice_bitcast_fusion), channel_id=1, replica_groups=mesh['dp'=16,'tensor'=2] {'dp'}, dimensions={0}, use_global_device_ids=true | all-gather | bytes 208896 | tf_op jit(solution)/shard_map/all_gather | solution.py:189
  664.8 6.6 fusion.66
  674.6 214.2 %all-reduce.7.cloned.1.call-done = (bf16[1024,3,512]{2,0,1:T(8,128)(2,1)}, bf16[512,1024]{1,0:T(8,128)(2,1)}, bf16[1024,2048]{1,0:T(8,128)(2,1)}, bf16[2048,1024]{1,0:T(8,128)(2,1)}) async-done(((bf16[1024,3,512]{2,0,1:T(8,128)(2,1)}, bf16[512,1024]{1,0:T(8,128)(2,1)}, bf16[1024,2048]{1,0:T(8,128)(2,1)}, bf16[2048,1024]{1,0:T(8,128)(2,1)}), (bf16[1024,3,512]{2,0,1:T(8,128)(2,1)}, ...) | async-done | bytes 12582928 | tf_op jit(solution)/shard_map/psum | solution.py:209
  (217 shorter events, 174.1 us)
Async XLA Ops:
  8.0 25.7 %copy-start = (bf16[1024,3,512]{2,0,1:T(8,128)(2,1)S(1)}, bf16[1024,3,512]{2,0,1:T(8,128)(2,1)}, u32[]{:S(2)}) copy-start(bf16[1024,3,512]{2,0,1:T(8,128)(2,1)} %param.24) | copy-start | bytes 9437188
  8.1 650.7 %all-reduce.5.cloned.1.call-start = ((), (), s32[]{:S(2)}) async-start(), calls=%async_computation.2 | async-start | bytes 663552
  12.0 141.3 %copy-start.25 = (f32[1360]{0:T(1024)}, f32[1360]{0:T(1024)S(1)}, u32[]{:S(2)}) copy-start(f32[1360]{0:T(1024)S(1)} %broadcast_multiply_fusion.5) | copy-start | bytes 16324
  14.7 139.2 %copy-start.28 = (f32[1360]{0:T(1024)}, f32[1360]{0:T(1024)S(1)}, u32[]{:S(2)}) copy-start(f32[1360]{0:T(1024)S(1)} %add_rsqrt_fusion.3) | copy-start | bytes 16324
  21.2 11.1 %copy-start.23 = (bf16[32,1024]{1,0:T(8,128)(2,1)}, bf16[32,1024]{1,0:T(8,128)(2,1)S(1)}, u32[]{:S(2)}) copy-start(bf16[32,1024]{1,0:T(8,128)(2,1)S(1)} %all_gather.15) | copy-start | bytes 196612
  29.5 11.1 %copy-start.32 = (f32[2,1024]{1,0:T(2,128)}, f32[2,1024]{1,0:T(2,128)S(1)}, u32[]{:S(2)}) copy-start(f32[2,1024]{1,0:T(2,128)S(1)} %get-tuple-element.53) | copy-start | bytes 24580
  67.3 22.4 %copy-start.30 = (f32[8]{0:T(128)}, f32[8]{0:T(128)S(1)}, u32[]{:S(2)}) copy-start(f32[8]{0:T(128)S(1)} %exp.22) | copy-start | bytes 100
  89.6 16.8 %copy-start.11 = (f32[2,680,8]{1,2,0:T(8,128)}, f32[2,680,8]{1,2,0:T(8,128)S(1)}, u32[]{:S(2)}) copy-start(f32[2,680,8]{1,2,0:T(8,128)S(1)} %get-tuple-element.68) | copy-start | bytes 130564
  89.6 16.8 %copy-start.18 = (f32[2,680,8]{1,2,0:T(8,128)}, f32[2,680,8]{1,2,0:T(8,128)S(1)}, u32[]{:S(2)}) copy-start(f32[2,680,8]{1,2,0:T(8,128)S(1)} %get-tuple-element.67) | copy-start | bytes 130564
  89.7 16.8 %copy-start.8 = (pred[2,680,680]{1,2,0:T(8,128)(4,1)S(1)}, pred[2,680,680]{1,2,0:T(8,128)(4,1)}, u32[]{:S(2)}) copy-start(pred[2,680,680]{1,2,0:T(8,128)(4,1)} %broadcast_compare_fusion) | copy-start | bytes 2774404
  151.2 60.4 %collective-permute-start = (bf16[1360,1024]{1,0:T(8,128)(2,1)}, bf16[1360,1024]{1,0:T(8,128)(2,1)}, u32[]{:S(2)}, u32[]{:S(2)}) collective-permute-start(bf16[1360,1024]{1,0:T(8,128)(2,1)} %convolution_convert_fusion.4), channel_id=1, source_target_pairs={{0,1},{1,0},{2,3},{3,2},{4,5},{5,4},{6,7},{7,6},{8,9},{9,8},{10,11... | collective-permute-start | bytes 8355848 | tf_op jit(solution)/shard_map/ppermute | solution.py:14
  243.0 130.2 %collective-permute-start.1 = (bf16[1360,1024]{1,0:T(8,128)(2,1)}, bf16[1360,1024]{1,0:T(8,128)(2,1)}, u32[]{:S(2)}, u32[]{:S(2)}) collective-permute-start(bf16[1360,1024]{1,0:T(8,128)(2,1)} %convolution_convert_fusion.1), channel_id=1, source_target_pairs={{0,1},{1,0},{2,3},{3,2},{4,5},{5,4},{6,7},{7,6},{8,9},{9,8},{10,11... | collective-permute-start | bytes 8355848 | tf_op jit(solution)/shard_map/ppermute | solution.py:14
  271.6 90.7 %collective-permute-start.2 = (bf16[1360,1024]{1,0:T(8,128)(2,1)}, bf16[1360,1024]{1,0:T(8,128)(2,1)}, u32[]{:S(2)}, u32[]{:S(2)}) collective-permute-start(bf16[1360,1024]{1,0:T(8,128)(2,1)} %convolution_convert_fusion), channel_id=1, source_target_pairs={{0,1},{1,0},{2,3},{3,2},{4,5},{5,4},{6,7},{7,6},{8,9},{9,8},{10,11... | collective-permute-start | bytes 8355848 | tf_op jit(solution)/shard_map/ppermute | solution.py:14
  362.3 11.0 %slice-start = ((s8[5570560]{0:T(1024)(128)(4,1)}), s8[4194304]{0:T(1024)(128)(4,1)S(1)}, s32[]{:S(2)}) async-start(s8[5570560]{0:T(1024)(128)(4,1)} %bitcast.169), calls=%async_computation.4 | async-start | bytes 8388608
  373.2 12.9 %copy-start.47 = (bf16[512,1024]{1,0:T(8,128)(2,1)S(1)}, bf16[512,1024]{1,0:T(8,128)(2,1)}, u32[]{:S(2)}) copy-start(bf16[512,1024]{1,0:T(8,128)(2,1)} %param.28) | copy-start | bytes 3145732
  446.8 28.4 %copy-start.12 = (f32[2,680,8]{1,2,0:T(8,128)S(1)}, f32[2,680,8]{1,2,0:T(8,128)}, u32[]{:S(2)}) copy-start(f32[2,680,8]{1,2,0:T(8,128)} %copy-done.11) | copy-start | bytes 130564
  446.8 28.4 %copy-start.31 = (f32[8]{0:T(128)S(1)}, f32[8]{0:T(128)}, u32[]{:S(2)}) copy-start(f32[8]{0:T(128)} %copy-done.30) | copy-start | bytes 100
  475.2 11.5 %copy-start.5 = (f32[2,680,1,8,64]{1,4,3,0,2:T(8,128)S(1)}, f32[2,680,1,8,64]{1,4,3,0,2:T(8,128)}, u32[]{:S(2)}) copy-start(f32[2,680,1,8,64]{1,4,3,0,2:T(8,128)} %copy.106) | copy-start | bytes 8355844
  475.2 11.5 %copy-start.7 = (f32[2,680,1,8,64]{1,4,3,0,2:T(8,128)S(1)}, f32[2,680,1,8,64]{1,4,3,0,2:T(8,128)}, u32[]{:S(2)}) copy-start(f32[2,680,1,8,64]{1,4,3,0,2:T(8,128)} %copy.107) | copy-start | bytes 8355844
  475.2 11.5 %copy-start.19 = (f32[2,680,8]{1,2,0:T(8,128)S(1)}, f32[2,680,8]{1,2,0:T(8,128)}, u32[]{:S(2)}) copy-start(f32[2,680,8]{1,2,0:T(8,128)} %copy-done.18) | copy-start | bytes 130564
  486.7 10.5 %copy-start.20 = (bf16[2,680,8,64]{1,3,2,0:T(8,128)(2,1)S(1)}, bf16[2,680,8,64]{1,3,2,0:T(8,128)(2,1)}, u32[]{:S(2)}) copy-start(bf16[2,680,8,64]{1,3,2,0:T(8,128)(2,1)} %fusion.48) | copy-start | bytes 4177924
  542.3 15.9 %copy-start.37 = (f32[1024]{0:T(1024)S(1)}, f32[1024]{0:T(1024)}, u32[]{:S(2)}) copy-start(f32[1024]{0:T(1024)} %get-tuple-element.29) | copy-start | bytes 12292
  542.3 15.9 %copy-start.38 = (f32[2048]{0:T(1024)S(1)}, f32[2048]{0:T(1024)}, u32[]{:S(2)}) copy-start(f32[2048]{0:T(1024)} %get-tuple-element.31) | copy-start | bytes 24580
  542.3 58.7 %collective-permute-start.3 = (bf16[1360,1024]{1,0:T(8,128)(2,1)}, bf16[1360,1024]{1,0:T(8,128)(2,1)}, u32[]{:S(2)}, u32[]{:S(2)}) collective-permute-start(bf16[1360,1024]{1,0:T(8,128)(2,1)} %bitcast_convert_fusion), channel_id=1, source_target_pairs={{0,1},{1,0},{2,3},{3,2},{4,5},{5,4},{6,7},{7,6},{8,9},{9,8},{10,11... | collective-permute-start | bytes 8355848 | tf_op jit(solution)/shard_map/ppermute | solution.py:14
  559.5 41.4 %copy-start.33 = (f32[2,1024]{1,0:T(2,128)S(1)}, f32[2,1024]{1,0:T(2,128)}, u32[]{:S(2)}) copy-start(f32[2,1024]{1,0:T(2,128)} %copy-done.32) | copy-start | bytes 24580
  559.5 111.9 %reduce-scatter.2.cloned.1.call-start = ((), (), s32[]{:S(2)}) async-start(), calls=%async_computation.1 | async-start | bytes 196608 | tf_op jit(solution)/shard_map/reduce_scatter | solution.py:200
  569.1 35.1 %copy-start.4 = (bf16[1360,1024]{1,0:T(8,128)(2,1)S(1)}, bf16[1360,1024]{1,0:T(8,128)(2,1)}, u32[]{:S(2)}) copy-start(bf16[1360,1024]{1,0:T(8,128)(2,1)} %param.17) | copy-start | bytes 8355844
  569.1 35.1 %copy-start.26 = (f32[1360]{0:T(1024)S(1)}, f32[1360]{0:T(1024)}, u32[]{:S(2)}) copy-start(f32[1360]{0:T(1024)} %copy-done.25) | copy-start | bytes 16324
  569.1 35.1 %copy-start.29 = (f32[1360]{0:T(1024)S(1)}, f32[1360]{0:T(1024)}, u32[]{:S(2)}) copy-start(f32[1360]{0:T(1024)} %copy-done.28) | copy-start | bytes 16324
  600.9 9.8 %slice-start.2 = ((s8[5570560]{0:T(1024)(128)(4,1)}), s8[4194304]{0:T(1024)(128)(4,1)S(1)}, s32[]{:S(2)}) async-start(s8[5570560]{0:T(1024)(128)(4,1)} %bitcast.174), calls=%async_computation.6 | async-start | bytes 8388608
  604.2 12.1 %slice-start.4 = ((s8[5570560]{0:T(1024)(128)(4,1)}), s8[4194304]{0:T(1024)(128)(4,1)S(1)}, s32[]{:S(2)}) async-start(s8[5570560]{0:T(1024)(128)(4,1)} %bitcast.176), calls=%async_computation.8 | async-start | bytes 8388608
  653.3 235.5 %all-reduce.7.cloned.1.call-start = ((), (), s32[]{:S(2)}) async-start(), calls=%async_computation.3 | async-start | bytes 25165824 | tf_op jit(solution)/shard_map/psum | solution.py:209
  (31 other events, 204.8 us)
Sparse Core Ops, SparseCore 0:
  559.6 89.7 all-reduce.4
  659.3 229.5 all-reduce.6
Sparse Core Ops, SparseCore 1:
  653.4 7.6 reduce-scatter.1

commit v2 on v1

v2 whole, which is shorter than its diff:
```python
from functools import partial

import jax
import jax.numpy as jnp
from jax import lax
from jax.experimental import pallas as pl
from jax.experimental.pallas import tpu as pltpu
from jax.sharding import PartitionSpec as P

epsilon = 1e-06
highest = lax.Precision.HIGHEST
CHUNKS = 4

def padded(length):
    return -(-length // 256) * 256, -(-length // (16 * CHUNKS)) * 16

def head_sums(values, low_half):
    first = jnp.sum(jnp.where(low_half, values, 0.0), axis=-1, keepdims=True)
    second = jnp.sum(jnp.where(low_half, 0.0, values), axis=-1, keepdims=True)
    return first, second

def unit_heads(raw, low_half):
    first, second = head_sums(raw * raw, low_half)
    inv = jnp.where(low_half, lax.rsqrt(first + epsilon), lax.rsqrt(second + epsilon))
    return raw * inv, inv

def lane_facts(length):
    lane = lax.broadcasted_iota(jnp.int32, (length, 128), 1)
    return lane < 64, lane & 63

def fill(ref, value):
    rows = value.shape[0]
    ref[:rows, :] = value.astype(ref.dtype)
    ref[rows:, :] = jnp.zeros((ref.shape[0] - rows, ref.shape[1]), ref.dtype)

def fwd_kernel(qkv_ref, sid_ref, growth_ref, out_ref, q_s, k_s, v_s):
    f32, bf16 = jnp.float32, jnp.bfloat16
    length = out_ref.shape[0]
    cols, step = padded(length)
    low_half, slot = lane_facts(length)
    sid = sid_ref[0]
    query, _ = unit_heads(qkv_ref[0, 0], low_half)
    key, _ = unit_heads(qkv_ref[1, 0], low_half)
    query = query * growth_ref[...]
    value = qkv_ref[2, 0]
    hide = jnp.where((slot > sid) & (slot < 16), -1e30, 0.0)
    own = jnp.where(slot == sid, 1.0, 0.0)
    for head in range(2):
        mine = low_half if head == 0 else ~low_half
        fill(q_s.at[head], jnp.where(mine, query, hide))
        fill(k_s.at[head], jnp.where(mine, key, own))
        fill(v_s.at[head], jnp.where(mine, value, 1.0))
    for chunk in range(CHUNKS):
        first = chunk * step
        rows = min(step, length - first)
        parts = []
        for head in range(2):
            scores = lax.dot_general(q_s[head, first : first + step, :], k_s[head], (((1,), (1,)), ((), ())), preferred_element_type=f32)
            weights = jnp.exp(scores).astype(bf16)
            parts.append(jnp.dot(weights, v_s[head], preferred_element_type=f32))
        half = low_half[:1]
        total = jnp.where(half, parts[1], parts[0])
        mixed = jnp.where(half, parts[0], parts[1]) / pltpu.roll(total, 64, 1)
        out_ref[first : first + rows, :] = mixed[:rows].astype(bf16)

def bwd_kernel(qkv_ref, sid_ref, growth_ref, dout_ref, dqkv_ref, sums_ref,
               q_s, k_s, v_s, do_s, qp_s, kp_s, dop_s, dst_s, weight_s, product_s):
    f32, bf16 = jnp.float32, jnp.bfloat16
    length = dout_ref.shape[0]
    cols, step = padded(length)
    low_half, slot = lane_facts(length)
    sid = sid_ref[0]
    query_unit, query_inv = unit_heads(qkv_ref[0, 0], low_half)
    key_unit, key_inv = unit_heads(qkv_ref[1, 0], low_half)
    query = query_unit * growth_ref[...]
    value = qkv_ref[2, 0]
    dout = dout_ref[...].astype(f32)
    hide = jnp.where((slot > sid) & (slot < 16), -1e30, 0.0)
    own = jnp.where(slot == sid, 1.0, 0.0)
    fill(qp_s, query)
    fill(kp_s, key_unit)
    fill(dop_s, dout)
    fill(v_s, value)
    for head in range(2):
        mine = low_half if head == 0 else ~low_half
        fill(q_s.at[head], jnp.where(mine, query, hide))
        fill(k_s.at[head], jnp.where(mine, key_unit, own))
        fill(do_s.at[head], jnp.where(mine, dout, 0.0))
    half = low_half[:1]
    d_key, d_value, d_query = [], [], []
    nt = (((1,), (1,)), ((), ()))
    for head in range(2):
        dks, dvs = [], []
        total, inner = jnp.zeros((1, cols), f32), jnp.zeros((1, cols), f32)
        for chunk in range(CHUNKS):
            rows = slice(chunk * step, (chunk + 1) * step)
            scores = lax.dot_general(k_s[head, rows, :], q_s[head], nt, preferred_element_type=f32)
            weights = jnp.exp(scores)
            if (chunk + 1) * step > length:
                row = lax.broadcasted_iota(jnp.int32, (step, cols), 0)
                weights = jnp.where(row < length - chunk * step, weights, 0.0)
            d_probs = lax.dot_general(v_s[rows, :], do_s[head], nt, preferred_element_type=f32)
            product = weights * d_probs
            weight_s[rows, :] = weights
            product_s[rows, :] = product
            total = total + jnp.sum(weights, axis=0, keepdims=True)
            inner = inner + jnp.sum(product, axis=0, keepdims=True)
        inv = 1.0 / total
        inner = inner * inv
        for chunk in range(CHUNKS):
            rows = slice(chunk * step, (chunk + 1) * step)
            probs = weight_s[rows, :] * inv
            d_scores = (product_s[rows, :] * inv - probs * inner).astype(bf16)
            dst_s[rows, :] = d_scores
            dvs.append(jnp.dot(probs.astype(bf16), dop_s[...], preferred_element_type=f32))
            dks.append(jnp.dot(d_scores, qp_s[...], preferred_element_type=f32))
        if CHUNKS * step < cols:
            dst_s[CHUNKS * step :, :] = jnp.zeros((cols - CHUNKS * step, cols), bf16)
        d_query.append(lax.dot_general(dst_s[...], kp_s[...], (((0,), (0,)), ((), ())), preferred_element_type=f32))
        d_key.append(jnp.concatenate(dks, axis=0))
        d_value.append(jnp.concatenate(dvs, axis=0))
    pick = lambda pair: jnp.where(half, pair[0], pair[1])[:length]
    d_query, d_key, d_value = pick(d_query), pick(d_key), pick(d_value)
    sums_ref[0:1, :] = jnp.sum(d_query * query, axis=0, keepdims=True)

    def back(d_unit, unit, inv):
        first, second = head_sums(d_unit * unit, low_half)
        return inv * (d_unit - unit * jnp.where(low_half, first, second))

    d_query = back(d_query * growth_ref[...], query_unit, query_inv).astype(bf16)
    d_key = back(d_key, key_unit, key_inv).astype(bf16)
    d_value = d_value.astype(bf16)
    dqkv_ref[0] = d_query
    dqkv_ref[1] = d_key
    dqkv_ref[2] = d_value
    sums_ref[1:2, :] = jnp.sum(d_query.astype(f32), axis=0, keepdims=True)
    sums_ref[2:3, :] = jnp.sum(d_value.astype(f32), axis=0, keepdims=True)
    sums_ref[3:8, :] = jnp.zeros((5, 128), f32)


def attention(qkv, sid, growth, image):
    _, _, length, width = qkv.shape
    cols, _ = padded(length)
    n = width // 64 * length * length
    return pl.pallas_call(
        fwd_kernel,
        grid=(width // 128,),
        in_specs=[
            pl.BlockSpec((3, 1, length, 128), lambda h: (0, image, 0, h)),
            pl.BlockSpec((1, length, 1), lambda h: (image, 0, 0)),
            pl.BlockSpec((1, 128), lambda h: (0, h)),
        ],
        out_specs=pl.BlockSpec((length, 128), lambda h: (0, h)),
        out_shape=jax.ShapeDtypeStruct((length, width), jnp.bfloat16),
        scratch_shapes=[pltpu.VMEM((2, cols, 128), jnp.bfloat16)] * 3,
        cost_estimate=pl.CostEstimate(flops=16 * 64 * n, transcendentals=n, bytes_accessed=14 * length * width),
        compiler_params=pltpu.CompilerParams(vmem_limit_bytes=48 << 20),
        name="attend",
    )(qkv, sid, growth)


def attention_back(qkv, sid, growth, dout, image):
    _, _, length, width = qkv.shape
    cols, step = padded(length)
    n = width // 64 * length * length
    two = pltpu.VMEM((2, cols, 128), jnp.bfloat16)
    one = pltpu.VMEM((cols, 128), jnp.bfloat16)
    wide = pltpu.VMEM((CHUNKS * step, cols), jnp.float32)
    return pl.pallas_call(
        bwd_kernel,
        grid=(width // 128,),
        in_specs=[
            pl.BlockSpec((3, 1, length, 128), lambda h: (0, image, 0, h)),
            pl.BlockSpec((1, length, 1), lambda h: (image, 0, 0)),
            pl.BlockSpec((1, 128), lambda h: (0, h)),
            pl.BlockSpec((length, 128), lambda h: (0, h)),
        ],
        out_specs=[pl.BlockSpec((3, length, 128), lambda h: (0, 0, h)), pl.BlockSpec((8, 128), lambda h: (0, h))],
        out_shape=[
            jax.ShapeDtypeStruct((3, length, width), jnp.bfloat16),
            jax.ShapeDtypeStruct((8, width), jnp.float32),
        ],
        scratch_shapes=[two, two, one, two, one, one, one, pltpu.VMEM((cols, cols), jnp.bfloat16), wide, wide],
        cost_estimate=pl.CostEstimate(flops=40 * 64 * n, transcendentals=n, bytes_accessed=20 * length * width),
        compiler_params=pltpu.CompilerParams(vmem_limit_bytes=56 << 20),
        name="attend_back",
    )(qkv, sid, growth, dout)


def after(value, *others):
    return lax.optimization_barrier((value, *others))[0]


def tensor_pair():
    return lax.axis_size("tensor") == 2


def tensor_swap(part):
    return lax.ppermute(part, "tensor", [(0, 1), (1, 0)])


def tensor_sum(part, *late):
    if tensor_pair():
        other = tensor_swap(part)
        if late:
            other = after(other, *late)
        return part.astype(jnp.float32) + other.astype(jnp.float32)
    return lax.psum(part, "tensor").astype(jnp.float32)


def joined(part, other, first, axis):
    return jnp.concatenate([jnp.where(first, part, other), jnp.where(first, other, part)], axis=axis)


def tensor_gather(part, axis):
    if tensor_pair():
        return joined(part, tensor_swap(part), lax.axis_index("tensor") == 0, axis)
    return lax.all_gather(part, "tensor", axis=axis, tiled=True)


def tensor_scatter(part):
    if tensor_pair():
        half = part.shape[1] // 2
        me = lax.axis_index("tensor")
        mine = lax.dynamic_slice_in_dim(part, me * half, half, 1)
        return mine + tensor_swap(lax.dynamic_slice_in_dim(part, (1 - me) * half, half, 1))
    return lax.psum_scatter(part, "tensor", scatter_dimension=1, tiled=True)


def grad_sum(make, shape, axis, pieces=1):
    bf16, f32 = jnp.bfloat16, jnp.float32
    rows = shape[axis]
    if lax.axis_size("dp") != 16:
        return lax.psum(make(0, rows).astype(bf16), "dp").astype(f32)
    index = lax.axis_index("dp")
    low, high, line = index % 2, index // 2 % 2, index // 4
    half, quarter = rows // 2, rows // 4
    cut = partial(lax.dynamic_slice_in_dim, axis=axis)
    swap = lambda value, bit: lax.ppermute(value, "dp", [(i, i ^ bit) for i in range(16)])

    def hop(value, moves):
        return lax.ppermute(value, "dp", [(4 * a + k, 4 * b + k) for a, b in moves for k in range(4)])

    theirs = make((1 - low) * half, half).astype(bf16)
    got = swap(theirs, 1)
    mine = make(low * half, half).astype(bf16)
    add = lambda first: (cut(mine, first, quarter).astype(f32) + cut(got, first, quarter).astype(f32)).astype(bf16)
    got_high = swap(add((1 - high) * quarter), 2)
    part = (add(high * quarter).astype(f32) + got_high.astype(f32)).astype(bf16)
    inner = (line == 1) | (line == 2)
    sums = []
    for piece in jnp.split(part, pieces, axis=axis):
        piece = (piece.astype(f32) + hop(piece, [(0, 1), (3, 2)]).astype(f32)).astype(bf16)
        piece = (piece.astype(f32) + hop(piece, [(1, 2), (2, 1)]).astype(f32)).astype(bf16)
        sums.append(jnp.where(inner, piece, hop(piece, [(1, 0), (2, 3)])))
    total = jnp.concatenate(sums, axis=axis) if pieces > 1 else sums[0]
    total = joined(total, swap(total, 2), high == 0, axis)
    return joined(total, swap(total, 1), low == 0, axis).astype(f32)


def layer_stats(values):
    center = values - jnp.mean(values, axis=-1, keepdims=True)
    inv_std = lax.rsqrt(jnp.mean(center * center, axis=-1, keepdims=True) + epsilon)
    return (center * inv_std, inv_std)


def layer_back(d_normed, normed, inv_std):
    first_mean = jnp.mean(d_normed, axis=-1, keepdims=True)
    second_mean = jnp.mean(d_normed * normed, axis=-1, keepdims=True)
    return inv_std * (d_normed - first_mean - normed * second_mean)


def per_device(
    tokens,
    d_out,
    labels,
    scale_ids,
    class_table,
    ada_weight,
    ada_bias,
    qkv_weight,
    q_bias,
    v_bias,
    qk_scale,
    proj_weight,
    proj_bias,
    fc1_weight,
    fc1_bias,
    fc2_weight,
    fc2_bias,
):
    f32 = jnp.float32
    bf16 = jnp.bfloat16
    dot = partial(jnp.dot, preferred_element_type=f32)
    ein = partial(jnp.einsum, preferred_element_type=f32)
    images, length = scale_ids.shape
    width = tokens.shape[1]
    classes = class_table.shape[0]
    heads_here = qk_scale.shape[0]
    local_width = qkv_weight.shape[2]
    head_size = local_width // heads_here
    mod_width = ada_weight.shape[1]
    every = range(images)
    rows = [slice(i * length, (i + 1) * length) for i in every]
    first_image = lax.axis_index("dp") * images

    class_ids = jnp.arange(classes, dtype=jnp.int32)
    pick_all = labels[:, None] == class_ids[None, :]
    cond_cols = dot(pick_all.astype(bf16), class_table)
    cond_all = tensor_gather(cond_cols.astype(bf16), 1)
    act_all = jax.nn.silu(cond_all.astype(f32)).astype(bf16)
    act_mine = lax.dynamic_slice_in_dim(act_all, first_image, images)
    mod_cols = dot(act_mine, ada_weight) + ada_bias.astype(f32)
    modul = tensor_gather(mod_cols, 1)
    proj_full = tensor_gather(after(proj_weight, modul), 0)
    gain_one, gain_two, scale_one, scale_two, shift_one, shift_two = [
        [modul[i : i + 1, member * width : (member + 1) * width] for i in every] for member in range(6)
    ]
    inputs = [tokens[rows[i]].astype(f32) for i in every]
    d_result = [d_out[rows[i]].astype(f32) for i in every]

    sid = scale_ids[:, :, None]
    growth = jnp.repeat(jnp.exp(qk_scale), head_size)[None]
    normed_one, inv_one = zip(*[layer_stats(inputs[i]) for i in every])
    hidden_one = jnp.concatenate(
        [(normed_one[i] * (1.0 + scale_one[i]) + shift_one[i]).astype(bf16) for i in every], axis=0
    )
    bias_stack = jnp.stack([q_bias.astype(f32), jnp.zeros(q_bias.shape, f32), v_bias.astype(f32)])
    qkv = ein("rd,dpc->prc", hidden_one, qkv_weight) + bias_stack[:, None, :]
    qkv = qkv.reshape(3, images, length, local_width)

    gelu_tanh = partial(jax.nn.gelu, approximate=True)
    attn, branch_one, middle, normed_two, inv_two = [], [], [], [], []
    hidden_two, pre_act, d_pre, d_hidden_two, parts = [], [], [], [], []
    d_branch_two = jnp.concatenate([(gain_two[i] * d_result[i]).astype(bf16) for i in every], axis=0)
    for i in every:
        attn.append(attention(qkv, sid, growth, i))
    for i in every:
        branch_one.append(dot(tensor_gather(attn[i], 1), proj_full) + proj_bias.astype(f32))
        middle.append(inputs[i] + gain_one[i] * branch_one[i])
        normed, inv = layer_stats(middle[i])
        normed_two.append(normed)
        inv_two.append(inv)
        hidden_two.append((normed * (1.0 + scale_two[i]) + shift_two[i]).astype(bf16))
        pre_act.append(dot(hidden_two[i], fc1_weight) + fc1_bias.astype(f32))
        d_mlp = ein("rd,fd->rf", d_branch_two[rows[i]], fc2_weight)
        gelu_value, gelu_pull = jax.vjp(gelu_tanh, pre_act[i])
        d_pre.append(gelu_pull(d_mlp)[0].astype(bf16))
        parts.append(ein("rf,df->rd", d_pre[i], fc1_weight).astype(bf16))
        d_hidden_two.append(tensor_sum(parts[i]))
    mlp_low = jnp.concatenate([gelu_tanh(pre_act[i]).astype(bf16) for i in every], axis=0)
    mlp_low = after(mlp_low, parts[-1])
    hidden_two = after(jnp.concatenate(hidden_two, axis=0), parts[-1])
    d_pre_all = after(jnp.concatenate(d_pre, axis=0), parts[-1])
    cols = partial(lax.dynamic_slice_in_dim, axis=1)
    grad_fc2 = grad_sum(lambda a, n: ein("rf,rd->fd", cols(mlp_low, a, n), d_branch_two), fc2_weight.shape, 0)
    grad_fc1 = grad_sum(lambda a, n: ein("rd,rf->df", cols(hidden_two, a, n), d_pre_all), fc1_weight.shape, 0)
    grad_fc2_bias = jnp.sum(d_branch_two.astype(f32), axis=0)
    grad_fc1_bias = jnp.sum(d_pre_all.astype(f32), axis=0)
    parts_two = [dot(mlp_low[rows[i]], fc2_weight).astype(bf16) for i in every]
    d_middle, d_branch_one, d_qkv, sums, d_hidden_one = [], [], [], [], []
    for i in every:
        d_middle.append(
            d_result[i] + layer_back(d_hidden_two[i] * (1.0 + scale_two[i]), normed_two[i], inv_two[i])
        )
        d_branch_one.append((gain_one[i] * d_middle[i]).astype(bf16))
        d_attn = ein("rd,cd->rc", d_branch_one[i], proj_weight).astype(bf16)
        d_qkv_i, sums_i = attention_back(qkv, sid, growth, d_attn, i)
        d_qkv.append(d_qkv_i)
        sums.append(sums_i)
        d_hidden_one.append(tensor_sum(ein("prc,dpc->rd", d_qkv_i, qkv_weight).astype(bf16)))
    branch_two = [tensor_sum(parts_two[i], d_qkv[-1]) + fc2_bias.astype(f32) for i in every]
    d_branch_one = jnp.concatenate(d_branch_one, axis=0)
    attn = jnp.concatenate(attn, axis=0)
    grad_proj = grad_sum(lambda a, n: ein("rc,rd->cd", cols(attn, a, n), d_branch_one), proj_weight.shape, 0)
    grad_proj_bias = jnp.sum(d_branch_one.astype(f32), axis=0)
    d_qkv = jnp.concatenate(d_qkv, axis=1)
    grad_qkv = grad_sum(
        lambda a, n: ein("rd,prc->pdc", cols(hidden_one, a, n), d_qkv), (3, width, local_width), 1, 2
    )
    grad_qkv = jnp.transpose(grad_qkv, (1, 0, 2))
    sums = sum(sums)
    grad_scale = jnp.sum(sums[0].reshape(heads_here, head_size), axis=1)
    grad_q_bias, grad_v_bias = sums[1], sums[2]
    result = jnp.concatenate(
        [(middle[i] + gain_two[i] * branch_two[i]).astype(bf16) for i in every], axis=0
    )
    d_tokens, d_modul = [], []
    for i in every:
        back = layer_back(d_hidden_one[i] * (1.0 + scale_one[i]), normed_one[i], inv_one[i])
        d_tokens.append((d_middle[i] + back).astype(bf16))
        d_modul.append(
            jnp.concatenate(
                [
                    jnp.sum(d_middle[i] * branch_one[i], axis=0),
                    jnp.sum(d_result[i] * branch_two[i], axis=0),
                    jnp.sum(d_hidden_one[i] * normed_one[i], axis=0),
                    jnp.sum(d_hidden_two[i] * normed_two[i], axis=0),
                    jnp.sum(d_hidden_one[i], axis=0),
                    jnp.sum(d_hidden_two[i], axis=0),
                ]
            ).astype(bf16)
        )
    d_tokens = jnp.concatenate(d_tokens, axis=0)
    col_start = lax.axis_index("tensor") * mod_width
    dmod_cols = lax.dynamic_slice_in_dim(jnp.stack(d_modul), col_start, mod_width, 1)
    dmod_all = lax.all_gather(dmod_cols, "dp", axis=0, tiled=True)
    small = [grad_q_bias, grad_v_bias, grad_scale, grad_proj_bias, grad_fc1_bias, grad_fc2_bias]
    sizes = [item.shape[0] for item in small]
    padding = -sum(sizes) % 1024
    packed = jnp.concatenate([*small, jnp.zeros((padding,), f32)]).reshape(1, -1, 128)
    packed = jnp.sum(lax.all_gather(packed, "dp", axis=0, tiled=True), axis=0).reshape(-1)
    ends = [sum(sizes[: k + 1]) for k in range(len(sizes))]
    grad_q_bias, grad_v_bias, grad_scale, grad_proj_bias, grad_fc1_bias, grad_fc2_bias = [
        packed[e - n : e] for e, n in zip(ends, sizes)
    ]
    d_act_part = ein("ic,dc->id", dmod_all, ada_weight)
    d_act_cols = tensor_scatter(d_act_part)
    silu_value, silu_pull = jax.vjp(jax.nn.silu, cond_cols)
    d_cond = silu_pull(d_act_cols)[0]
    grad_table = ein("in,ic->nc", pick_all.astype(f32), d_cond, precision=highest)
    grad_ada = ein("id,ic->dc", act_all, dmod_all)
    grad_ada_bias = jnp.sum(dmod_all.astype(f32), axis=0)
    return (
        result,
        d_tokens,
        grad_table,
        grad_ada,
        grad_ada_bias,
        grad_qkv,
        grad_q_bias,
        grad_v_bias,
        grad_scale,
        grad_proj,
        grad_proj_bias,
        grad_fc1,
        grad_fc1_bias,
        grad_fc2,
        grad_fc2_bias,
    )


def solution(mesh):
    return jax.shard_map(
        per_device,
        mesh=mesh,
        in_specs=(
            P("dp", None),
            P("dp", None),
            P(),
            P("dp", None),
            P(None, "tensor"),
            P(None, "tensor"),
            P("tensor"),
            P(None, None, "tensor"),
            P("tensor"),
            P("tensor"),
            P("tensor"),
            P("tensor", None),
            P(),
            P(None, "tensor"),
            P("tensor"),
            P("tensor", None),
            P(),
        ),
        out_specs=(
            P("dp", None),
            P("dp", None),
            P(None, "tensor"),
            P(None, "tensor"),
            P("tensor"),
            P(None, None, "tensor"),
            P("tensor"),
            P("tensor"),
            P("tensor"),
            P("tensor", None),
            P(),
            P(None, "tensor"),
            P("tensor"),
            P("tensor", None),
            P(),
        ),
        check_vma=False,
    )
```

time: 920 us -> 647 us (0.70)
  waiting for transfers between devices: 376 us -> 211 us
  matrix products: 232 us -> 130 us
  local copies, waits for them, and re-layouts: 107 us -> 28.1 us
  Pallas kernels: 0 us -> 67.8 us
  other arithmetic: 144 us -> 98.3 us
  starting transfers between devices: 5.94 us -> 40.2 us
  blocking collectives: 31.9 us -> 64.3 us
  between operations: 17.4 us -> 2.66 us
    psum x1 -> x0, waiting for transfers between devices: 214 us -> none  [per_device(): lax.psum(grad_qkv.astype(bf16), 'dp').astype(f32)]
    dot_general x23 -> x28, matrix products: 232 us -> 130 us  [the longest x2 22.7 us: per_device(): d_mlp = ein('rd,fd->rf', d_branch_two[rows[i]], fc2_weight)]
    pallas_call x0 -> x4, Pallas kernels: none -> 67.8 us  [the longest x2 45.8 us: attention_back(): pl.pallas_call(bwd_kernel, grid=(width // 128,), in_specs=[pl.BlockSpec((...]
    ppermute x4 -> x43, waiting for transfers between devices: 162 us -> 211 us  [the longest x15 100 us: hop(): lax.ppermute(value, 'dp', [(4 * a + k, 4 * b + k) for a, b in moves for k...]
    ppermute x4 -> x43, starting transfers between devices: 5.53 us -> 40.2 us  [the longest x15 19.1 us: hop(): lax.ppermute(value, 'dp', [(4 * a + k, 4 * b + k) for a, b in moves for k...]
    another operation x7 -> x2, local copies, waits for them, and re-layouts: 26.2 us -> 0.16 us  [the longest x1 0.08 us: per_device(): growth = jnp.repeat(jnp.exp(qk_scale), head_size)[None]]
    reduce_sum x9 -> x8, other arithmetic: 46.4 us -> 22.4 us  [the longest x1 5.87 us: per_device(): jnp.sum(d_hidden_one[i] * normed_one[i], axis=0)]
    reshape x3 -> x0, local copies, waits for them, and re-layouts: 21.6 us -> none  [the longest x1 12.9 us: per_device(): qkv_val = qkv_val.reshape(images, length, 3, heads_here, head_size)]
  transfers between devices with their start and end apart: 7 -> 43, of which waited for: 4 -> 17; matrix products, arithmetic and copies ran while one was open for 14% -> 30% of each run, Pallas kernels for 0% -> 11%
where the time goes in v2:
time: 647 us; the launch traced here: 643 us
  waiting for transfers between devices  211 us (33%)
  matrix products  130 us (20%)
  other arithmetic  98.3 us (15%)
  Pallas kernels  67.8 us (10%)
  blocking collectives  64.3 us (10%)
  starting transfers between devices  40.2 us (6%)
  local copies, waits for them, and re-layouts  28.1 us (4%)
    ppermute x15, waiting for transfers between devices, hop(): lax.ppermute(value, 'dp', [(4 * a + k, 4 * b + k) for a, b in moves for k...  100 us
    ppermute x12, waiting for transfers between devices, tensor_swap(): return lax.ppermute(part, 'tensor', [(0, 1), (1, 0)])  73.9 us
    pallas_call x2, Pallas kernels, attention_back(): pl.pallas_call(bwd_kernel, grid=(width // 128,), in_specs=[pl.BlockSpec((...  45.8 us
    all_gather x1, blocking collectives, per_device(): dmod_all = lax.all_gather(dmod_cols, 'dp', axis=0, tiled=True)  41.2 us
    ppermute x16, waiting for transfers between devices, grad_sum(): lax.ppermute(value, 'dp', [(i, i ^ bit) for i in range(16)])  37.2 us
    all_gather x1, blocking collectives, per_device(): lax.all_gather(packed, 'dp', axis=0, tiled=True)  23.1 us
    dot_general x2, matrix products, per_device(): d_mlp = ein('rd,fd->rf', d_branch_two[rows[i]], fc2_weight)  22.7 us
    pallas_call x2, Pallas kernels, attention(): pl.pallas_call(fwd_kernel, grid=(width // 128,), in_specs=[pl.BlockSpec((...  22 us
  transfers between devices with their start and end apart: 43, of which 17 were waited for; matrix products, arithmetic and copies ran while one was open for 30% of the time, Pallas kernels for 11%

profile of v2, /device:TPU:0, one launch (start us, length us, event | category | flops | bytes accessed | tf_op | source)
XLA Modules:
  0.0 642.8 jit_solution(8548257454436893006)
XLA Ops:
  19.1 12.2 %collective-permute-done.1 = f32[2,3072]{1,0:T(2,128)S(1)} collective-permute-done((f32[2,3072]{1,0:T(2,128)S(1)}, f32[2,3072]{1,0:T(2,128)S(1)}, u32[]{:S(2)}, u32[]{:S(2)}) %collective-permute-start.1) | collective-permute-done | bytes 24608 | tf_op jit(solution)/shard_map/ppermute | solution.py:199
  34.4 8.0 %convolution_add_fusion = f32[1360,3,512]{2,0,1:T(8,128)} fusion(bf16[1024,3,512]{2,0,1:T(8,128)(2,1)S(1)} %copy-done, f32[3,512]{1,0:T(4,128)S(1)} %pad_maximum_fusion.20, bf16[680,1024]{1,0:T(8,128)(2,1)S(1)} %get-tuple-element.85, bf16[680,1024]{1,0:T(8,128)(2,1)S(1)} %get-tuple-element.84), kind=kOutput, calls=%fused_computation.26 | convolution fusion | flops 4285849600 | bytes 14292992 | tf_op jit(solution)/shard_map/rd,dpc->prc/dot_general | solution.py:329
  42.3 10.8 %attend.3 = bf16[680,512]{1,0:T(8,128)(2,1)S(1)} custom-call(f32[3,2,680,512]{3,2,1,0:T(8,128)} %bitcast.123, s32[2,680,1]{2,1,0:T(8,128)S(1)} %copy-done.5, f32[1,512]{1,0:T(1,128)S(1)} %broadcast_in_dim_reshape.3.growth_ref), custom_call_target="tpu_custom_call" | custom-call | flops 3787980800 | bytes 4874240 | tf_op jit(solution)/shard_map/attend/pallas_call | solution.py:145
  53.2 11.1 %attend.2 = bf16[680,512]{1,0:T(8,128)(2,1)S(1)} custom-call(f32[3,2,680,512]{3,2,1,0:T(8,128)} %bitcast.124, s32[2,680,1]{2,1,0:T(8,128)S(1)} %copy-done.5, f32[1,512]{1,0:T(1,128)S(1)} %broadcast_in_dim_reshape.3.growth_ref), custom_call_target="tpu_custom_call" | custom-call | flops 3787980800 | bytes 4874240 | tf_op jit(solution)/shard_map/attend/pallas_call | solution.py:145
  68.7 5.2 fusion.156
  74.4 8.5 %collective-permute-done.4 = bf16[680,512]{1,0:T(8,128)(2,1)S(1)} collective-permute-done((bf16[680,512]{1,0:T(8,128)(2,1)S(1)}, bf16[680,512]{1,0:T(8,128)(2,1)S(1)}, u32[]{:S(2)}, u32[]{:S(2)}) %collective-permute-start.4) | collective-permute-done | bytes 696352 | tf_op jit(solution)/shard_map/ppermute | solution.py:199
  83.0 12.7 %collective-permute-done.2 = bf16[680,512]{1,0:T(8,128)(2,1)S(1)} collective-permute-done((bf16[680,512]{1,0:T(8,128)(2,1)S(1)}, bf16[680,512]{1,0:T(8,128)(2,1)S(1)}, u32[]{:S(2)}, u32[]{:S(2)}) %collective-permute-start.2) | collective-permute-done | bytes 696352 | tf_op jit(solution)/shard_map/ppermute | solution.py:199
  117.9 17.5 %fusion.6 = (bf16[680,2048]{1,0:T(8,128)(2,1)}, bf16[680,2048]{1,0:T(8,128)(2,1)}, bf16[680,2048]{1,0:T(8,128)(2,1)}, bf16[680,2048]{1,0:T(8,128)(2,1)}) fusion(f32[680,2048]{1,0:T(8,128)} %fusion.154, f32[2048]{0:T(1024)S(1)} %convert_element_type.428, f32[680,2048]{1,0:T(8,128)} %fusion.155, f32[680,2048]{1,0:T(8,128)} %fusion.156, ...), kind=kOutput, calls=%fused_computation.12 | convolution fusion | flops 2916188160 | bytes 33447936 | tf_op jit(solution)/shard_map/rd,fd->rf/dot_general | solution.py:346
  135.4 7.3 %convolution_convert_fusion.5 = bf16[680,1024]{1,0:T(8,128)(2,1)} fusion(bf16[680,2048]{1,0:T(8,128)(2,1)} %get-tuple-element.130, bf16[1024,2048]{1,0:T(8,128)(2,1)} %param.30), kind=kOutput, calls=%fused_computation.157 | convolution fusion | flops 2852823040 | bytes 8372224 | tf_op jit(solution)/shard_map/rf,df->rd/dot_general | solution.py:349
  143.7 6.0 pad_maximum_fusion
  149.8 7.3 %fusion.76 = bf16[680,1024]{1,0:T(8,128)(2,1)} fusion(bf16[2048,1024]{1,0:T(8,128)(2,1)} %param.32, bf16[1360,2048]{1,0:T(8,128)(2,1)} %pad_maximum_fusion), kind=kOutput, calls=%fused_computation.154 | convolution fusion | flops 2852823040 | bytes 8372224 | tf_op jit(solution)/shard_map/dot_general | solution.py:360
  165.4 6.1 pad_maximum_fusion.1
  196.4 40.4 %collective-permute-done.8 = bf16[680,1024]{1,0:T(8,128)(2,1)S(1)} collective-permute-done((bf16[680,1024]{1,0:T(8,128)(2,1)}, bf16[680,1024]{1,0:T(8,128)(2,1)S(1)}, u32[]{:S(2)}, u32[]{:S(2)}) %collective-permute-start.8) | collective-permute-done | bytes 1392672 | tf_op jit(solution)/shard_map/ppermute | solution.py:199
  241.8 5.7 multiply_reduce_fusion.3
  251.3 23.0 %attend_back.2 = (bf16[3,680,512]{2,1,0:T(8,128)(2,1)}, f32[8,512]{1,0:T(8,128)}) custom-call(f32[3,2,680,512]{3,2,1,0:T(8,128)} %bitcast.125, s32[2,680,1]{2,1,0:T(8,128)} %copy.38.sid_ref, f32[1,512]{1,0:T(1,128)} %copy-done.6, bf16[680,512]{1,0:T(8,128)(2,1)} %convolution_convert_fusion.7.dout_ref), custom_call_target="tpu_custom_call" | custom-call | flops 9469952000 | bytes 6963200 | tf_op jit(solution)/shard_map/attend_back/pallas_call | solution.py:169
  277.5 22.8 %attend_back.3 = (bf16[3,680,512]{2,1,0:T(8,128)(2,1)}, f32[8,512]{1,0:T(8,128)}) custom-call(f32[3,2,680,512]{3,2,1,0:T(8,128)} %bitcast.126, s32[2,680,1]{2,1,0:T(8,128)} %copy.38.sid_ref, f32[1,512]{1,0:T(1,128)} %copy-done.6, bf16[680,512]{1,0:T(8,128)(2,1)} %convolution_convert_fusion.6.dout_ref), custom_call_target="tpu_custom_call" | custom-call | flops 9469952000 | bytes 6963200 | tf_op jit(solution)/shard_map/attend_back/pallas_call | solution.py:169
  316.7 23.1 %all_gather.7 = f32[16,48,128]{2,1,0:T(8,128)S(1)} all-gather(f32[1,48,128]{2,1,0:T(8,128)} %bitcast.90), channel_id=1, replica_groups=mesh['dp'=16,'tensor'=2] {'dp'}, dimensions={0}, use_global_device_ids=true | all-gather | bytes 417792 | tf_op jit(solution)/shard_map/all_gather | solution.py:412
  362.3 6.2 collective-permute-done.23
  387.6 5.9 fusion.42
  395.9 5.4 fusion.41
  402.2 41.2 %all-gather = bf16[16,2,3072]{2,1,0:T(2,128)(2,1)S(1)} all-gather(bf16[1,2,3072]{2,1,0:T(2,128)(2,1)S(1)} %fusion.126), channel_id=1, replica_groups=mesh['dp'=16,'tensor'=2] {'dp'}, dimensions={0}, use_global_device_ids=true | all-gather | bytes 208896 | tf_op jit(solution)/shard_map/all_gather | solution.py:407
  445.1 7.5 %fusion.146 = f32[1024,3072]{1,0:T(8,128)} fusion(bf16[32,3072]{1,0:T(8,128)(2,1)S(1)} %reshape.307, bf16[32,512]{1,0:T(8,128)(2,1)} %copy-done.57, bf16[32,512]{1,0:T(8,128)(2,1)} %copy-done.56), kind=kOutput, calls=%fused_computation.315 | convolution fusion | flops 201621504 | bytes 12845056 | tf_op jit(solution)/shard_map/id,ic->dc/dot_general | solution.py:422
  457.6 7.2 %collective-permute-done.13 = bf16[3,256,512]{2,1,0:T(8,128)(2,1)S(1)} collective-permute-done((bf16[3,256,512]{2,1,0:T(8,128)(2,1)S(1)}, bf16[3,256,512]{2,1,0:T(8,128)(2,1)S(1)}, u32[]{:S(2)}, u32[]{:S(2)}) %collective-permute-start.13) | collective-permute-done | bytes 786464 | tf_op jit(solution)/shard_map/ppermute | solution.py:239
  477.8 11.7 %collective-permute-done.14 = bf16[3,128,512]{2,1,0:T(8,128)(2,1)S(1)} collective-permute-done((bf16[3,128,512]{2,1,0:T(8,128)(2,1)S(1)}, bf16[3,128,512]{2,1,0:T(8,128)(2,1)S(1)}, u32[]{:S(2)}, u32[]{:S(2)}) %collective-permute-start.14) | collective-permute-done | bytes 393248 | tf_op jit(solution)/shard_map/ppermute | solution.py:242
  489.5 8.4 %collective-permute-done.17 = bf16[3,128,512]{2,1,0:T(8,128)(2,1)S(1)} collective-permute-done((bf16[3,128,512]{2,1,0:T(8,128)(2,1)S(1)}, bf16[3,128,512]{2,1,0:T(8,128)(2,1)S(1)}, u32[]{:S(2)}, u32[]{:S(2)}) %collective-permute-start.17) | collective-permute-done | bytes 393248 | tf_op jit(solution)/shard_map/ppermute | solution.py:242
  502.5 17.0 %collective-permute-done.38 = bf16[512,1024]{1,0:T(8,128)(2,1)S(1)} collective-permute-done((bf16[512,1024]{1,0:T(8,128)(2,1)S(1)}, bf16[512,1024]{1,0:T(8,128)(2,1)S(1)}, u32[]{:S(2)}, u32[]{:S(2)}) %collective-permute-start.38) | collective-permute-done | bytes 1048608 | tf_op jit(solution)/shard_map/ppermute | solution.py:242
  525.5 9.8 %collective-permute-done.19 = bf16[3,128,512]{2,1,0:T(8,128)(2,1)S(1)} collective-permute-done((bf16[3,128,512]{2,1,0:T(8,128)(2,1)S(1)}, bf16[3,128,512]{2,1,0:T(8,128)(2,1)S(1)}, u32[]{:S(2)}, u32[]{:S(2)}) %collective-permute-start.19) | collective-permute-done | bytes 393248 | tf_op jit(solution)/shard_map/ppermute | solution.py:242
  536.2 20.6 %collective-permute-done.16 = bf16[3,128,512]{2,1,0:T(8,128)(2,1)S(1)} collective-permute-done((bf16[3,128,512]{2,1,0:T(8,128)(2,1)S(1)}, bf16[3,128,512]{2,1,0:T(8,128)(2,1)S(1)}, u32[]{:S(2)}, u32[]{:S(2)}) %collective-permute-start.16) | collective-permute-done | bytes 393248 | tf_op jit(solution)/shard_map/ppermute | solution.py:242
  559.1 20.2 %collective-permute-done.33 = bf16[256,2048]{1,0:T(8,128)(2,1)S(1)} collective-permute-done((bf16[256,2048]{1,0:T(8,128)(2,1)S(1)}, bf16[256,2048]{1,0:T(8,128)(2,1)S(1)}, u32[]{:S(2)}, u32[]{:S(2)}) %collective-permute-start.33) | collective-permute-done | bytes 1048608 | tf_op jit(solution)/shard_map/ppermute | solution.py:242
  583.7 12.1 %collective-permute-done.40 = bf16[512,1024]{1,0:T(8,128)(2,1)S(1)} collective-permute-done((bf16[512,1024]{1,0:T(8,128)(2,1)S(1)}, bf16[512,1024]{1,0:T(8,128)(2,1)S(1)}, u32[]{:S(2)}, u32[]{:S(2)}) %collective-permute-start.40) | collective-permute-done | bytes 1048608 | tf_op jit(solution)/shard_map/ppermute | solution.py:242
  599.8 5.2 collective-permute-done.27
  605.2 16.7 %collective-permute-done.41 = bf16[512,1024]{1,0:T(8,128)(2,1)S(1)} collective-permute-done((bf16[512,1024]{1,0:T(8,128)(2,1)S(1)}, bf16[512,1024]{1,0:T(8,128)(2,1)S(1)}, u32[]{:S(2)}, u32[]{:S(2)}) %collective-permute-start.41) | collective-permute-done | bytes 1048608 | tf_op jit(solution)/shard_map/ppermute | solution.py:239
  (402 shorter events, 217.1 us)
Async XLA Ops:
  6.0 89.8 %collective-permute-start.3 = (bf16[512,1024]{1,0:T(8,128)(2,1)}, bf16[512,1024]{1,0:T(8,128)(2,1)}, u32[]{:S(2)}, u32[]{:S(2)}) collective-permute-start(bf16[512,1024]{1,0:T(8,128)(2,1)} %param.28), channel_id=1, source_target_pairs={{0,1},{1,0},{2,3},{3,2},{4,5},{5,4},{6,7},{7,6},{8,9},{9,8},{10,11... | collective-permute-start | bytes 3145736 | tf_op jit(solution)/shard_map/ppermute | solution.py:199
  65.2 30.5 %collective-permute-start.2 = (bf16[680,512]{1,0:T(8,128)(2,1)S(1)}, bf16[680,512]{1,0:T(8,128)(2,1)S(1)}, u32[]{:S(2)}, u32[]{:S(2)}) collective-permute-start(bf16[680,512]{1,0:T(8,128)(2,1)S(1)} %attend.2), channel_id=1, source_target_pairs={{0,1},{1,0},{2,3},{3,2},{4,5},{5,4},{6,7},{7,6},{8,9},{9,8},{10,11... | collective-permute-start | bytes 2088968 | tf_op jit(solution)/shard_map/ppermute | solution.py:199
  142.7 95.7 %collective-permute-start.6 = (bf16[680,1024]{1,0:T(8,128)(2,1)}, bf16[680,1024]{1,0:T(8,128)(2,1)}, u32[]{:S(2)}, u32[]{:S(2)}) collective-permute-start(bf16[680,1024]{1,0:T(8,128)(2,1)} %convolution_convert_fusion.5), channel_id=1, source_target_pairs={{0,1},{1,0},{2,3},{3,2},{4,5},{5,4},{6,7},{7,6},{8,9},{9,8},{10,11... | collective-permute-start | bytes 4177928 | tf_op jit(solution)/shard_map/ppermute | solution.py:199
  173.4 127.6 %collective-permute-start.5 = (bf16[680,1024]{1,0:T(8,128)(2,1)}, bf16[680,1024]{1,0:T(8,128)(2,1)}, u32[]{:S(2)}, u32[]{:S(2)}) collective-permute-start(bf16[680,1024]{1,0:T(8,128)(2,1)} %fusion.76), channel_id=1, source_target_pairs={{0,1},{1,0},{2,3},{3,2},{4,5},{5,4},{6,7},{7,6},{8,9},{9,8},{10,11... | collective-permute-start | bytes 4177928 | tf_op jit(solution)/shard_map/ppermute | solution.py:199
  174.3 62.5 %collective-permute-start.8 = (bf16[680,1024]{1,0:T(8,128)(2,1)}, bf16[680,1024]{1,0:T(8,128)(2,1)S(1)}, u32[]{:S(2)}, u32[]{:S(2)}) collective-permute-start(bf16[680,1024]{1,0:T(8,128)(2,1)} %convolution_convert_fusion.4), channel_id=1, source_target_pairs={{0,1},{1,0},{2,3},{3,2},{4,5},{5,4},{6,7},{7,6},{8,9},{9,8},{10,11... | collective-permute-start | bytes 4177928 | tf_op jit(solution)/shard_map/ppermute | solution.py:199
  175.4 133.7 %collective-permute-start.7 = (bf16[680,1024]{1,0:T(8,128)(2,1)}, bf16[680,1024]{1,0:T(8,128)(2,1)}, u32[]{:S(2)}, u32[]{:S(2)}) collective-permute-start(bf16[680,1024]{1,0:T(8,128)(2,1)} %fusion.79), channel_id=1, source_target_pairs={{0,1},{1,0},{2,3},{3,2},{4,5},{5,4},{6,7},{7,6},{8,9},{9,8},{10,11... | collective-permute-start | bytes 4177928 | tf_op jit(solution)/shard_map/ppermute | solution.py:199
  182.0 194.7 %collective-permute-start.29 = (bf16[512,2048]{1,0:T(8,128)(2,1)}, bf16[512,2048]{1,0:T(8,128)(2,1)}, u32[]{:S(2)}, u32[]{:S(2)}) collective-permute-start(bf16[512,2048]{1,0:T(8,128)(2,1)} %convolution_convert_fusion), channel_id=1, source_target_pairs={{0,2},{2,0},{4,6},{6,4},{8,10},{10,8},{12,14},{14,12},{16,18},{18,... | collective-permute-start | bytes 6291464 | tf_op jit(solution)/shard_map/ppermute | solution.py:239
  236.8 143.6 %collective-permute-start.36 = (bf16[1024,1024]{1,0:T(8,128)(2,1)}, bf16[1024,1024]{1,0:T(8,128)(2,1)}, u32[]{:S(2)}, u32[]{:S(2)}) collective-permute-start(bf16[1024,1024]{1,0:T(8,128)(2,1)} %fusion.73), channel_id=1, source_target_pairs={{0,2},{2,0},{4,6},{6,4},{8,10},{10,8},{12,14},{14,12},{16,18},{18,... | collective-permute-start | bytes 6291464 | tf_op jit(solution)/shard_map/ppermute | solution.py:239
  309.1 76.8 %collective-permute-start.9 = (bf16[680,1024]{1,0:T(8,128)(2,1)}, bf16[680,1024]{1,0:T(8,128)(2,1)}, u32[]{:S(2)}, u32[]{:S(2)}) collective-permute-start(bf16[680,1024]{1,0:T(8,128)(2,1)} %bitcast_convert_fusion.1), channel_id=1, source_target_pairs={{0,1},{1,0},{2,3},{3,2},{4,5},{5,4},{6,7},{7,6},{8,9},{9,8},{10,11... | collective-permute-start | bytes 4177928 | tf_op jit(solution)/shard_map/ppermute | solution.py:199
  310.1 77.4 %collective-permute-start.10 = (bf16[680,1024]{1,0:T(8,128)(2,1)}, bf16[680,1024]{1,0:T(8,128)(2,1)}, u32[]{:S(2)}, u32[]{:S(2)}) collective-permute-start(bf16[680,1024]{1,0:T(8,128)(2,1)} %bitcast_convert_fusion), channel_id=1, source_target_pairs={{0,1},{1,0},{2,3},{3,2},{4,5},{5,4},{6,7},{7,6},{8,9},{9,8},{10,11... | collective-permute-start | bytes 4177928 | tf_op jit(solution)/shard_map/ppermute | solution.py:199
  376.6 66.8 %collective-permute-start.12 = (bf16[3,512,512]{2,1,0:T(8,128)(2,1)}, bf16[3,512,512]{2,1,0:T(8,128)(2,1)}, u32[]{:S(2)}, u32[]{:S(2)}) collective-permute-start(bf16[3,512,512]{2,1,0:T(8,128)(2,1)} %fusion.84), channel_id=1, source_target_pairs={{0,2},{2,0},{4,6},{6,4},{8,10},{10,8},{12,14},{14,12},{16,18},{18,... | collective-permute-start | bytes 4718600 | tf_op jit(solution)/shard_map/ppermute | solution.py:239
  380.5 72.2 %collective-permute-start.30 = (bf16[256,2048]{1,0:T(8,128)(2,1)}, bf16[256,2048]{1,0:T(8,128)(2,1)}, u32[]{:S(2)}, u32[]{:S(2)}) collective-permute-start(bf16[256,2048]{1,0:T(8,128)(2,1)} %add_convert_fusion.12), channel_id=1, source_target_pairs={{0,4},{2,6},{4,0},{6,2},{8,12},{10,14},{12,8},{14,10},{16,20},{18,... | collective-permute-start | bytes 3145736 | tf_op jit(solution)/shard_map/ppermute | solution.py:239
  383.6 90.3 %collective-permute-start.37 = (bf16[512,1024]{1,0:T(8,128)(2,1)}, bf16[512,1024]{1,0:T(8,128)(2,1)}, u32[]{:S(2)}, u32[]{:S(2)}) collective-permute-start(bf16[512,1024]{1,0:T(8,128)(2,1)} %add_convert_fusion.7), channel_id=1, source_target_pairs={{0,4},{2,6},{4,0},{6,2},{8,12},{10,14},{12,8},{14,10},{16,20},{18,... | collective-permute-start | bytes 3145736 | tf_op jit(solution)/shard_map/ppermute | solution.py:239
  385.9 194.6 %collective-permute-start.26 = (bf16[128,1024]{1,0:T(8,128)(2,1)}, bf16[128,1024]{1,0:T(8,128)(2,1)}, u32[]{:S(2)}, u32[]{:S(2)}) collective-permute-start(bf16[128,1024]{1,0:T(8,128)(2,1)} %add_convert_fusion.19), channel_id=1, source_target_pairs={{8,0},{10,2},{12,4},{14,6},{16,24},{18,26},{20,28},{22,30},{9,1},{... | collective-permute-start | bytes 786440 | tf_op jit(solution)/shard_map/ppermute | solution.py:242
  454.8 44.1 %collective-permute-start.31 = (bf16[256,2048]{1,0:T(8,128)(2,1)S(1)}, bf16[256,2048]{1,0:T(8,128)(2,1)S(1)}, u32[]{:S(2)}, u32[]{:S(2)}) collective-permute-start(bf16[256,2048]{1,0:T(8,128)(2,1)S(1)} %add_convert_fusion.11), channel_id=1, source_target_pairs={{0,8},{2,10},{4,12},{6,14},{24,16},{26,18},{28,20},{30,22},{1,9},{... | collective-permute-start | bytes 3145736 | tf_op jit(solution)/shard_map/ppermute | solution.py:242
  466.4 23.1 %collective-permute-start.14 = (bf16[3,128,512]{2,1,0:T(8,128)(2,1)S(1)}, bf16[3,128,512]{2,1,0:T(8,128)(2,1)S(1)}, u32[]{:S(2)}, u32[]{:S(2)}) collective-permute-start(bf16[3,128,512]{2,1,0:T(8,128)(2,1)S(1)} %get-tuple-element.102), channel_id=1, source_target_pairs={{0,8},{2,10},{4,12},{6,14},{24,16},{26,18},{28,20},{30,22},{1,9},{... | collective-permute-start | bytes 1179656 | tf_op jit(solution)/shard_map/ppermute | solution.py:242
  467.7 30.2 %collective-permute-start.17 = (bf16[3,128,512]{2,1,0:T(8,128)(2,1)S(1)}, bf16[3,128,512]{2,1,0:T(8,128)(2,1)S(1)}, u32[]{:S(2)}, u32[]{:S(2)}) collective-permute-start(bf16[3,128,512]{2,1,0:T(8,128)(2,1)S(1)} %get-tuple-element.103), channel_id=1, source_target_pairs={{0,8},{2,10},{4,12},{6,14},{24,16},{26,18},{28,20},{30,22},{1,9},{... | collective-permute-start | bytes 1179656 | tf_op jit(solution)/shard_map/ppermute | solution.py:242
  476.2 43.3 %collective-permute-start.38 = (bf16[512,1024]{1,0:T(8,128)(2,1)S(1)}, bf16[512,1024]{1,0:T(8,128)(2,1)S(1)}, u32[]{:S(2)}, u32[]{:S(2)}) collective-permute-start(bf16[512,1024]{1,0:T(8,128)(2,1)S(1)} %add_convert_fusion.6), channel_id=1, source_target_pairs={{0,8},{2,10},{4,12},{6,14},{24,16},{26,18},{28,20},{30,22},{1,9},{... | collective-permute-start | bytes 3145736 | tf_op jit(solution)/shard_map/ppermute | solution.py:242
  498.2 22.5 %collective-permute-start.18 = (bf16[3,128,512]{2,1,0:T(8,128)(2,1)S(1)}, bf16[3,128,512]{2,1,0:T(8,128)(2,1)S(1)}, u32[]{:S(2)}, u32[]{:S(2)}) collective-permute-start(bf16[3,128,512]{2,1,0:T(8,128)(2,1)S(1)} %get-tuple-element.101), channel_id=1, source_target_pairs={{8,16},{10,18},{12,20},{14,22},{16,8},{18,10},{20,12},{22,14},{9,1... | collective-permute-start | bytes 1179656 | tf_op jit(solution)/shard_map/ppermute | solution.py:242
  499.3 24.2 %collective-permute-start.32 = (bf16[256,2048]{1,0:T(8,128)(2,1)S(1)}, bf16[256,2048]{1,0:T(8,128)(2,1)S(1)}, u32[]{:S(2)}, u32[]{:S(2)}) collective-permute-start(bf16[256,2048]{1,0:T(8,128)(2,1)S(1)} %add_convert_fusion.10), channel_id=1, source_target_pairs={{8,16},{10,18},{12,20},{14,22},{16,8},{18,10},{20,12},{22,14},{9,1... | collective-permute-start | bytes 3145736 | tf_op jit(solution)/shard_map/ppermute | solution.py:242
  501.9 20.2 %collective-permute-start.15 = (bf16[3,128,512]{2,1,0:T(8,128)(2,1)S(1)}, bf16[3,128,512]{2,1,0:T(8,128)(2,1)S(1)}, u32[]{:S(2)}, u32[]{:S(2)}) collective-permute-start(bf16[3,128,512]{2,1,0:T(8,128)(2,1)S(1)} %get-tuple-element.100), channel_id=1, source_target_pairs={{8,16},{10,18},{12,20},{14,22},{16,8},{18,10},{20,12},{22,14},{9,1... | collective-permute-start | bytes 1179656 | tf_op jit(solution)/shard_map/ppermute | solution.py:242
  519.9 37.5 %collective-permute-start.39 = (bf16[512,1024]{1,0:T(8,128)(2,1)S(1)}, bf16[512,1024]{1,0:T(8,128)(2,1)S(1)}, u32[]{:S(2)}, u32[]{:S(2)}) collective-permute-start(bf16[512,1024]{1,0:T(8,128)(2,1)S(1)} %add_convert_fusion.5), channel_id=1, source_target_pairs={{8,16},{10,18},{12,20},{14,22},{16,8},{18,10},{20,12},{22,14},{9,1... | collective-permute-start | bytes 3145736 | tf_op jit(solution)/shard_map/ppermute | solution.py:242
  522.2 34.6 %collective-permute-start.16 = (bf16[3,128,512]{2,1,0:T(8,128)(2,1)S(1)}, bf16[3,128,512]{2,1,0:T(8,128)(2,1)S(1)}, u32[]{:S(2)}, u32[]{:S(2)}) collective-permute-start(bf16[3,128,512]{2,1,0:T(8,128)(2,1)S(1)} %add_convert_fusion.17), channel_id=1, source_target_pairs={{8,0},{10,2},{12,4},{14,6},{16,24},{18,26},{20,28},{22,30},{9,1},{... | collective-permute-start | bytes 1179656 | tf_op jit(solution)/shard_map/ppermute | solution.py:242
  523.9 55.4 %collective-permute-start.33 = (bf16[256,2048]{1,0:T(8,128)(2,1)S(1)}, bf16[256,2048]{1,0:T(8,128)(2,1)S(1)}, u32[]{:S(2)}, u32[]{:S(2)}) collective-permute-start(bf16[256,2048]{1,0:T(8,128)(2,1)S(1)} %add_convert_fusion.9), channel_id=1, source_target_pairs={{8,0},{10,2},{12,4},{14,6},{16,24},{18,26},{20,28},{22,30},{9,1},{... | collective-permute-start | bytes 3145736 | tf_op jit(solution)/shard_map/ppermute | solution.py:242
  535.3 87.0 %collective-permute-start.11 = (f32[32,512]{1,0:T(8,128)S(1)}, f32[32,512]{1,0:T(8,128)S(1)}, u32[]{:S(2)}, u32[]{:S(2)}) collective-permute-start(f32[32,512]{1,0:T(8,128)S(1)} %constant_dynamic-slice_fusion), channel_id=1, source_target_pairs={{0,1},{1,0},{2,3},{3,2},{4,5},{5,4},{6,7},{7,6},{8,9},{9,8},{10,11... | collective-permute-start | bytes 196616 | tf_op jit(solution)/shard_map/ppermute | solution.py:199
  556.9 26.3 %collective-permute-start.20 = (bf16[3,256,512]{2,1,0:T(8,128)(2,1)S(1)}, bf16[3,256,512]{2,1,0:T(8,128)(2,1)S(1)}, u32[]{:S(2)}, u32[]{:S(2)}) collective-permute-start(bf16[3,256,512]{2,1,0:T(8,128)(2,1)S(1)} %pad_maximum_fusion.18), channel_id=1, source_target_pairs={{0,4},{2,6},{4,0},{6,2},{8,12},{10,14},{12,8},{14,10},{16,20},{18,... | collective-permute-start | bytes 2359304 | tf_op jit(solution)/shard_map/ppermute | solution.py:239
  557.8 38.0 %collective-permute-start.40 = (bf16[512,1024]{1,0:T(8,128)(2,1)S(1)}, bf16[512,1024]{1,0:T(8,128)(2,1)S(1)}, u32[]{:S(2)}, u32[]{:S(2)}) collective-permute-start(bf16[512,1024]{1,0:T(8,128)(2,1)S(1)} %add_convert_fusion.4), channel_id=1, source_target_pairs={{8,0},{10,2},{12,4},{14,6},{16,24},{18,26},{20,28},{22,30},{9,1},{... | collective-permute-start | bytes 3145736 | tf_op jit(solution)/shard_map/ppermute | solution.py:242
  581.5 23.5 %collective-permute-start.27 = (bf16[128,1024]{1,0:T(8,128)(2,1)S(1)}, bf16[128,1024]{1,0:T(8,128)(2,1)S(1)}, u32[]{:S(2)}, u32[]{:S(2)}) collective-permute-start(bf16[128,1024]{1,0:T(8,128)(2,1)S(1)} %broadcast_select_fusion.24), channel_id=1, source_target_pairs={{0,4},{2,6},{4,0},{6,2},{8,12},{10,14},{12,8},{14,10},{16,20},{18,... | collective-permute-start | bytes 786440 | tf_op jit(solution)/shard_map/ppermute | solution.py:239
  583.6 43.4 %collective-permute-start.21 = (bf16[3,512,512]{2,1,0:T(8,128)(2,1)S(1)}, bf16[3,512,512]{2,1,0:T(8,128)(2,1)S(1)}, u32[]{:S(2)}, u32[]{:S(2)}) collective-permute-start(bf16[3,512,512]{2,1,0:T(8,128)(2,1)S(1)} %pad_maximum_fusion.11), channel_id=1, source_target_pairs={{0,2},{2,0},{4,6},{6,4},{8,10},{10,8},{12,14},{14,12},{16,18},{18,... | collective-permute-start | bytes 4718600 | tf_op jit(solution)/shard_map/ppermute | solution.py:239
  595.9 25.9 %collective-permute-start.41 = (bf16[512,1024]{1,0:T(8,128)(2,1)S(1)}, bf16[512,1024]{1,0:T(8,128)(2,1)S(1)}, u32[]{:S(2)}, u32[]{:S(2)}) collective-permute-start(bf16[512,1024]{1,0:T(8,128)(2,1)S(1)} %broadcast_select_fusion.6), channel_id=1, source_target_pairs={{0,4},{2,6},{4,0},{6,2},{8,12},{10,14},{12,8},{14,10},{16,20},{18,... | collective-permute-start | bytes 3145736 | tf_op jit(solution)/shard_map/ppermute | solution.py:239
  599.7 31.5 %collective-permute-start.35 = (bf16[512,2048]{1,0:T(8,128)(2,1)S(1)}, bf16[512,2048]{1,0:T(8,128)(2,1)S(1)}, u32[]{:S(2)}, u32[]{:S(2)}) collective-permute-start(bf16[512,2048]{1,0:T(8,128)(2,1)S(1)} %pad_maximum_fusion.9), channel_id=1, source_target_pairs={{0,2},{2,0},{4,6},{6,4},{8,10},{10,8},{12,14},{14,12},{16,18},{18,... | collective-permute-start | bytes 6291464 | tf_op jit(solution)/shard_map/ppermute | solution.py:239
  605.1 20.1 %collective-permute-start.28 = (bf16[256,1024]{1,0:T(8,128)(2,1)S(1)}, bf16[256,1024]{1,0:T(8,128)(2,1)S(1)}, u32[]{:S(2)}, u32[]{:S(2)}) collective-permute-start(bf16[256,1024]{1,0:T(8,128)(2,1)S(1)} %pad_maximum_fusion.19), channel_id=1, source_target_pairs={{0,2},{2,0},{4,6},{6,4},{8,10},{10,8},{12,14},{14,12},{16,18},{18,... | collective-permute-start | bytes 1572872 | tf_op jit(solution)/shard_map/ppermute | solution.py:239
  (104 other events, 1303.5 us)
